TPU v7x, 128 devices: a whole 4x4x4 slice. The times are simulated.
128 devices in a mesh: group: 8 (over x, core), dev: 16 (over y, z).
Axes of the slice: x: 4, y: 4, z: 4, core: 2. Of those that a mesh axis runs over, the one named last changes fastest.
Arguments:
- images: bfloat16 [16384, 1152], P(('group', 'dev')), may hold values from -1 to 1
- texts: bfloat16 [16384, 1152], P(('group', 'dev')), may hold values from -1 to 1
- lang_order: int32 [16384], P(('group', 'dev')), may hold values from 0 to 2047, as said below
- position: int32 [16384], P(('group', 'dev')), may hold values from 0 to 2047, as said below
- logit_scale: float32 [1], replicated, may hold values from 8 to 24
- logit_bias: float32 [1], replicated, may hold values from -4 to -1
Outputs:
- image_grad: float32 [16384, 1152], P(('group', 'dev'))
- text_grad: float32 [16384, 1152], P(('group', 'dev'))
- loss: float32 [1], replicated
Inputs may be any that keep to these rules, and one draw needn't show every extreme that they name: In each group of 2048 examples, lang_order is a permutation of the group-local indices; the 128 entries of one device name at most 16 examples held by any one device of the group, and exactly 16 for each device they name. position is the inverse of lang_order within each group.
All inputs are finite; a program needn't handle non-finite values.
Results may differ from a plain program's by a relative error of at most 0.00062.
Values may be sent and summed in bfloat16 or wider, within the bound.
A program may use at most 64 MiB of HBM per device.

v0:
```python
import jax
import jax.numpy as jnp
from jax import lax
from jax.sharding import Mesh
from jax.sharding import PartitionSpec as P

DEV = ("dev_0", "dev_1")
GROUP = ("group_0", "group_1")
GROUP_DEV = ("group_0", "group_1", "dev_0", "dev_1")


EPSILON = 1e-06


def from_behind(array, axis, by):
    count = lax.axis_size(axis)
    return lax.ppermute(array, axis, [(i, (i + by) % count) for i in range(count)])


def over_axes(array, axes):
    for axis in axes:
        array = lax.psum(array, axis)
    return array


def normalize(values):
    wide = values.astype(jnp.float32)
    recip = lax.rsqrt(jnp.sum(wide * wide, axis=1, keepdims=True) + EPSILON)
    return (wide * recip, recip)


def project_back(unit, recip, grad):
    return recip * (grad - unit * jnp.sum(unit * grad, axis=1, keepdims=True))


def slot_table(peer, rank_key, slot_count, slot_depth):
    same = (peer[None, :] == peer[:, None]) & (rank_key[None, :] < rank_key[:, None])
    rank = jnp.sum(same.astype(jnp.int32), axis=1)
    slot = peer * slot_depth + rank
    return jnp.arange(slot_count, dtype=jnp.int32)[:, None] == slot[None, :]


def block_terms(img_block, stretch, img_ids, txt_ids, scale, bias):
    logits = (
        scale
        * lax.dot_general(
            img_block, stretch, (((1,), (1,)), ((), ())), preferred_element_type=jnp.float32
        )
        + bias
    )
    sign = jnp.where(img_ids[:, None] == txt_ids[None, :], jnp.float32(1.0), jnp.float32(-1.0))
    loss_part = jnp.sum(-jax.nn.log_sigmoid(sign * logits))
    coeff = (-sign * jax.nn.sigmoid(-sign * logits)).astype(jnp.bfloat16)
    dimg_part = jnp.dot(coeff, stretch, preferred_element_type=jnp.float32)
    dtext_part = lax.dot_general(
        coeff, img_block, (((0,), (0,)), ((), ())), preferred_element_type=jnp.float32
    )
    return (loss_part, dimg_part, dtext_part)


def per_device(images, texts, lang_order, position, logit_scale, logit_bias):
    row_count, width_count = images.shape
    dev_count = lax.axis_size(DEV)
    group_count = lax.axis_size(GROUP)
    slot_depth = row_count // 8
    slot_count = dev_count * slot_depth
    scale = logit_scale[0]
    bias = logit_bias[0]
    group_index = lax.axis_index(GROUP)
    dev_index = lax.axis_index(DEV)
    local_ids = jnp.arange(row_count, dtype=jnp.int32)
    img_unit, img_recip = normalize(images)
    img_half = img_unit.astype(jnp.bfloat16)
    txt_unit, txt_recip = normalize(texts)
    txt_half = txt_unit.astype(jnp.bfloat16)
    send_table = slot_table(lang_order // row_count, local_ids, slot_count, slot_depth)
    recv_table = slot_table(position // row_count, position % row_count, slot_count, slot_depth)
    outgoing = jnp.dot(
        send_table.astype(jnp.bfloat16), txt_half, preferred_element_type=jnp.float32
    ).astype(jnp.bfloat16)
    arrived = lax.all_to_all(outgoing, DEV, split_axis=0, concat_axis=0, tiled=True)
    batch_text = lax.dot_general(
        recv_table.astype(jnp.bfloat16),
        arrived,
        (((0,), (0,)), ((), ())),
        preferred_element_type=jnp.float32,
    ).astype(jnp.bfloat16)
    zero_grad = jnp.zeros((row_count, width_count), jnp.float32)
    zero_loss = jnp.zeros((), jnp.float32)
    img_block = lax.all_gather(img_half, DEV, axis=0, tiled=True)
    img_ids = group_index * dev_count * row_count + jnp.arange(
        dev_count * row_count, dtype=jnp.int32
    )

    def turn_group(turn_index, carry):
        stretch, stretch_grad, dimg_acc, loss_acc = carry
        source = (group_index - turn_index) % group_count
        txt_ids = (source * dev_count + dev_index) * row_count + local_ids
        loss_part, dimg_part, dtext_part = block_terms(
            img_block, stretch, img_ids, txt_ids, scale, bias
        )
        stretch = from_behind(stretch, GROUP, 1)
        stretch_grad = from_behind(stretch_grad + dtext_part, GROUP, 1)
        return (stretch, stretch_grad, dimg_acc + dimg_part, loss_acc + loss_part)

    init = (
        batch_text,
        zero_grad,
        jnp.zeros((img_block.shape[0], width_count), jnp.float32),
        zero_loss,
    )
    stretch, stretch_grad, dimg_acc, loss_acc = lax.fori_loop(0, group_count, turn_group, init)
    dimg_own = lax.psum_scatter(dimg_acc, DEV, scatter_dimension=0, tiled=True)
    loss_sum = over_axes(loss_acc, GROUP_DEV)
    total = jnp.float32(row_count * dev_count * group_count)
    loss = (loss_sum / (total * total)).reshape(1)
    dimg = scale * dimg_own
    dtext = scale * stretch_grad
    going_back = jnp.dot(
        recv_table.astype(jnp.float32),
        dtext,
        precision=lax.Precision.HIGHEST,
        preferred_element_type=jnp.float32,
    )
    returned = lax.all_to_all(going_back, DEV, split_axis=0, concat_axis=0, tiled=True)
    dtext_lang = lax.dot_general(
        send_table.astype(jnp.float32),
        returned,
        (((0,), (0,)), ((), ())),
        precision=lax.Precision.HIGHEST,
        preferred_element_type=jnp.float32,
    )
    image_grad = project_back(img_unit, img_recip, dimg)
    text_grad = project_back(txt_unit, txt_recip, dtext_lang)
    return (image_grad, text_grad, loss)


def solution(mesh):
    finer = Mesh(mesh.devices.reshape(4, 2, 4, 4), ("group_0", "group_1", "dev_0", "dev_1"))
    return jax.shard_map(
        per_device,
        mesh=finer,
        in_specs=(P(GROUP_DEV, None), P(GROUP_DEV, None), P(GROUP_DEV), P(GROUP_DEV), P(), P()),
        out_specs=(P(GROUP_DEV, None), P(GROUP_DEV, None), P()),
        check_vma=False,
    )
```

profile of v0, /device:TPU:0, one launch (start us, length us, event | category | flops | bytes accessed | tf_op | source)
XLA Modules:
  0.0 324.8 jit_solution(8393622069548913051)
XLA Ops:
  14.9 8.2 %all-to-all-start = ((bf16[16,16,1152]{2,1,0:T(8,128)(2,1)}), bf16[16,16,1152]{2,1,0:T(8,128)(2,1)S(1)}, u32[]{:S(2)}, u32[]{:S(2)}) async-start(bf16[16,16,1152]{2,1,0:T(8,128)(2,1)} %bitcast.1), calls=%async_computation | async-start | bytes 1179648 | tf_op jit(solution)/shard_map/all_to_all | solution.py:81
  24.0 14.2 %all-to-all-done = bf16[16,16,1152]{2,1,0:T(8,128)(2,1)S(1)} async-done(((bf16[16,16,1152]{2,1,0:T(8,128)(2,1)}), bf16[16,16,1152]{2,1,0:T(8,128)(2,1)S(1)}, u32[]{:S(2)}, u32[]{:S(2)}) %all-to-all-start) | async-done | bytes 589856 | tf_op jit(solution)/shard_map/all_to_all | solution.py:81
  38.5 32.6 %all-gather.2.cloned.1.call-done = bf16[2048,1152]{1,0:T(8,128)(2,1)} async-done(((bf16[128,1152]{1,0:T(8,128)(2,1)}), bf16[2048,1152]{1,0:T(8,128)(2,1)}) %all-gather.2.cloned.1.call-update) | async-done | bytes 4718608 | tf_op jit(solution)/shard_map/all_gather | solution.py:90
  71.1 146.7 %while.22 = (s32[]{:T(128)}, bf16[128,1152]{1,0:T(8,128)(2,1)S(1)}, f32[128,1152]{1,0:T(8,128)S(1)}, f32[2048,1152]{1,0:T(8,128)}, f32[]{:T(128)}, /*index=5*/s3...) while((s32[]{:T(128)}, bf16[128,1152]{1,0:T(8,128)(2,1)S(1)}, ...), condition=%wide.region_6.7_spmd.clone, body=%wide.region_4.6_spmd.clone.sunk | while | flops 1824934016 | bytes 56265160 | solution.py:112
  71.2 6.2 %fusion.60 = (f32[]{:T(128)}, f32[2048,128]{1,0:T(8,128)S(1)}) fusion(s32[128]{0:T(128)S(1)} %iota_add_fusion.4, s32[2048]{0:T(1024)S(1)} %iota_add_fusion.5, f32[]{:T(128)} %get-tuple-element.478, bf16[2048,1152]{1,0:T(8,128)(2,1)} %get-tuple-element.477, bf16[128,1152]{1,0:T(8,128)(2,1)S(1)} %copy.15, f32[]{:T(128)} %get-tuple-element.476), kind=kOutput, calls=%fused_computation.16.clone.1 | convolution fusion | flops 607387648 | bytes 6070796 | tf_op jit(solution)/shard_map/while/body/eval_jaxpr/dot_general | solution.py:46
  80.5 4.5 %convolution_add_fusion.5 = f32[2048,1152]{1,0:T(8,128)} fusion(bf16[128,1152]{1,0:T(8,128)(2,1)S(1)} %copy.15, f32[2048,1152]{1,0:T(8,128)} %get-tuple-element.455, pred[]{:T(512)S(6)} %compare.9, f32[2048,128]{1,0:T(8,128)S(1)} %get-tuple-element.433, s32[128]{0:T(128)S(1)} %iota_add_fusion.4, s32[2048]{0:T(1024)S(1)} %iota_add_fusion.5), kind=kOutput, calls=%fused_computation.2.clone.1 | convolution fusion | flops 611057664 | bytes 20226560 | tf_op jit(solution)/shard_map/while/body/eval_jaxpr/dot_general | solution.py:54
  85.6 3.9 %collective-permute-done.1 = f32[128,1152]{1,0:T(8,128)S(1)} collective-permute-done((f32[128,1152]{1,0:T(8,128)S(1)}, f32[128,1152]{1,0:T(8,128)S(1)}, u32[]{:S(2)}, u32[]{:S(2)}) %collective-permute-start.1) | collective-permute-done | bytes 589856 | tf_op jit(solution)/shard_map/while/body/eval_jaxpr/ppermute | solution.py:17
  89.6 6.2 %fusion.60 = (f32[]{:T(128)}, f32[2048,128]{1,0:T(8,128)S(1)}) fusion(s32[128]{0:T(128)S(1)} %iota_add_fusion.4, s32[2048]{0:T(1024)S(1)} %iota_add_fusion.5, f32[]{:T(128)} %get-tuple-element.478, bf16[2048,1152]{1,0:T(8,128)(2,1)} %get-tuple-element.477, bf16[128,1152]{1,0:T(8,128)(2,1)S(1)} %copy.15, f32[]{:T(128)} %get-tuple-element.476), kind=kOutput, calls=%fused_computation.16.clone.1 | convolution fusion | flops 607387648 | bytes 6070796 | tf_op jit(solution)/shard_map/while/body/eval_jaxpr/dot_general | solution.py:46
  97.6 6.8 %convolution_add_fusion.5 = f32[2048,1152]{1,0:T(8,128)} fusion(bf16[128,1152]{1,0:T(8,128)(2,1)S(1)} %copy.15, f32[2048,1152]{1,0:T(8,128)} %get-tuple-element.455, pred[]{:T(512)S(6)} %compare.9, f32[2048,128]{1,0:T(8,128)S(1)} %get-tuple-element.433, s32[128]{0:T(128)S(1)} %iota_add_fusion.4, s32[2048]{0:T(1024)S(1)} %iota_add_fusion.5), kind=kOutput, calls=%fused_computation.2.clone.1 | convolution fusion | flops 611057664 | bytes 20226560 | tf_op jit(solution)/shard_map/while/body/eval_jaxpr/dot_general | solution.py:54
  107.9 6.2 %fusion.60 = (f32[]{:T(128)}, f32[2048,128]{1,0:T(8,128)S(1)}) fusion(s32[128]{0:T(128)S(1)} %iota_add_fusion.4, s32[2048]{0:T(1024)S(1)} %iota_add_fusion.5, f32[]{:T(128)} %get-tuple-element.478, bf16[2048,1152]{1,0:T(8,128)(2,1)} %get-tuple-element.477, bf16[128,1152]{1,0:T(8,128)(2,1)S(1)} %copy.15, f32[]{:T(128)} %get-tuple-element.476), kind=kOutput, calls=%fused_computation.16.clone.1 | convolution fusion | flops 607387648 | bytes 6070796 | tf_op jit(solution)/shard_map/while/body/eval_jaxpr/dot_general | solution.py:46
  115.7 6.8 %convolution_add_fusion.5 = f32[2048,1152]{1,0:T(8,128)} fusion(bf16[128,1152]{1,0:T(8,128)(2,1)S(1)} %copy.15, f32[2048,1152]{1,0:T(8,128)} %get-tuple-element.455, pred[]{:T(512)S(6)} %compare.9, f32[2048,128]{1,0:T(8,128)S(1)} %get-tuple-element.433, s32[128]{0:T(128)S(1)} %iota_add_fusion.4, s32[2048]{0:T(1024)S(1)} %iota_add_fusion.5), kind=kOutput, calls=%fused_computation.2.clone.1 | convolution fusion | flops 611057664 | bytes 20226560 | tf_op jit(solution)/shard_map/while/body/eval_jaxpr/dot_general | solution.py:54
  123.1 3.0 collective-permute-done.1
  126.3 6.2 %fusion.60 = (f32[]{:T(128)}, f32[2048,128]{1,0:T(8,128)S(1)}) fusion(s32[128]{0:T(128)S(1)} %iota_add_fusion.4, s32[2048]{0:T(1024)S(1)} %iota_add_fusion.5, f32[]{:T(128)} %get-tuple-element.478, bf16[2048,1152]{1,0:T(8,128)(2,1)} %get-tuple-element.477, bf16[128,1152]{1,0:T(8,128)(2,1)S(1)} %copy.15, f32[]{:T(128)} %get-tuple-element.476), kind=kOutput, calls=%fused_computation.16.clone.1 | convolution fusion | flops 607387648 | bytes 6070796 | tf_op jit(solution)/shard_map/while/body/eval_jaxpr/dot_general | solution.py:46
  134.0 6.8 %convolution_add_fusion.5 = f32[2048,1152]{1,0:T(8,128)} fusion(bf16[128,1152]{1,0:T(8,128)(2,1)S(1)} %copy.15, f32[2048,1152]{1,0:T(8,128)} %get-tuple-element.455, pred[]{:T(512)S(6)} %compare.9, f32[2048,128]{1,0:T(8,128)S(1)} %get-tuple-element.433, s32[128]{0:T(128)S(1)} %iota_add_fusion.4, s32[2048]{0:T(1024)S(1)} %iota_add_fusion.5), kind=kOutput, calls=%fused_computation.2.clone.1 | convolution fusion | flops 611057664 | bytes 20226560 | tf_op jit(solution)/shard_map/while/body/eval_jaxpr/dot_general | solution.py:54
  141.5 3.0 collective-permute-done.1
  144.6 6.2 %fusion.60 = (f32[]{:T(128)}, f32[2048,128]{1,0:T(8,128)S(1)}) fusion(s32[128]{0:T(128)S(1)} %iota_add_fusion.4, s32[2048]{0:T(1024)S(1)} %iota_add_fusion.5, f32[]{:T(128)} %get-tuple-element.478, bf16[2048,1152]{1,0:T(8,128)(2,1)} %get-tuple-element.477, bf16[128,1152]{1,0:T(8,128)(2,1)S(1)} %copy.15, f32[]{:T(128)} %get-tuple-element.476), kind=kOutput, calls=%fused_computation.16.clone.1 | convolution fusion | flops 607387648 | bytes 6070796 | tf_op jit(solution)/shard_map/while/body/eval_jaxpr/dot_general | solution.py:46
  152.3 6.8 %convolution_add_fusion.5 = f32[2048,1152]{1,0:T(8,128)} fusion(bf16[128,1152]{1,0:T(8,128)(2,1)S(1)} %copy.15, f32[2048,1152]{1,0:T(8,128)} %get-tuple-element.455, pred[]{:T(512)S(6)} %compare.9, f32[2048,128]{1,0:T(8,128)S(1)} %get-tuple-element.433, s32[128]{0:T(128)S(1)} %iota_add_fusion.4, s32[2048]{0:T(1024)S(1)} %iota_add_fusion.5), kind=kOutput, calls=%fused_computation.2.clone.1 | convolution fusion | flops 611057664 | bytes 20226560 | tf_op jit(solution)/shard_map/while/body/eval_jaxpr/dot_general | solution.py:54
  159.8 3.0 collective-permute-done.1
  162.9 6.2 %fusion.60 = (f32[]{:T(128)}, f32[2048,128]{1,0:T(8,128)S(1)}) fusion(s32[128]{0:T(128)S(1)} %iota_add_fusion.4, s32[2048]{0:T(1024)S(1)} %iota_add_fusion.5, f32[]{:T(128)} %get-tuple-element.478, bf16[2048,1152]{1,0:T(8,128)(2,1)} %get-tuple-element.477, bf16[128,1152]{1,0:T(8,128)(2,1)S(1)} %copy.15, f32[]{:T(128)} %get-tuple-element.476), kind=kOutput, calls=%fused_computation.16.clone.1 | convolution fusion | flops 607387648 | bytes 6070796 | tf_op jit(solution)/shard_map/while/body/eval_jaxpr/dot_general | solution.py:46
  170.7 6.8 %convolution_add_fusion.5 = f32[2048,1152]{1,0:T(8,128)} fusion(bf16[128,1152]{1,0:T(8,128)(2,1)S(1)} %copy.15, f32[2048,1152]{1,0:T(8,128)} %get-tuple-element.455, pred[]{:T(512)S(6)} %compare.9, f32[2048,128]{1,0:T(8,128)S(1)} %get-tuple-element.433, s32[128]{0:T(128)S(1)} %iota_add_fusion.4, s32[2048]{0:T(1024)S(1)} %iota_add_fusion.5), kind=kOutput, calls=%fused_computation.2.clone.1 | convolution fusion | flops 611057664 | bytes 20226560 | tf_op jit(solution)/shard_map/while/body/eval_jaxpr/dot_general | solution.py:54
  178.2 3.0 collective-permute-done.1
  181.3 6.2 %fusion.60 = (f32[]{:T(128)}, f32[2048,128]{1,0:T(8,128)S(1)}) fusion(s32[128]{0:T(128)S(1)} %iota_add_fusion.4, s32[2048]{0:T(1024)S(1)} %iota_add_fusion.5, f32[]{:T(128)} %get-tuple-element.478, bf16[2048,1152]{1,0:T(8,128)(2,1)} %get-tuple-element.477, bf16[128,1152]{1,0:T(8,128)(2,1)S(1)} %copy.15, f32[]{:T(128)} %get-tuple-element.476), kind=kOutput, calls=%fused_computation.16.clone.1 | convolution fusion | flops 607387648 | bytes 6070796 | tf_op jit(solution)/shard_map/while/body/eval_jaxpr/dot_general | solution.py:46
  189.0 6.8 %convolution_add_fusion.5 = f32[2048,1152]{1,0:T(8,128)} fusion(bf16[128,1152]{1,0:T(8,128)(2,1)S(1)} %copy.15, f32[2048,1152]{1,0:T(8,128)} %get-tuple-element.455, pred[]{:T(512)S(6)} %compare.9, f32[2048,128]{1,0:T(8,128)S(1)} %get-tuple-element.433, s32[128]{0:T(128)S(1)} %iota_add_fusion.4, s32[2048]{0:T(1024)S(1)} %iota_add_fusion.5), kind=kOutput, calls=%fused_computation.2.clone.1 | convolution fusion | flops 611057664 | bytes 20226560 | tf_op jit(solution)/shard_map/while/body/eval_jaxpr/dot_general | solution.py:54
  196.5 3.0 collective-permute-done.1
  199.6 6.2 %fusion.60 = (f32[]{:T(128)}, f32[2048,128]{1,0:T(8,128)S(1)}) fusion(s32[128]{0:T(128)S(1)} %iota_add_fusion.4, s32[2048]{0:T(1024)S(1)} %iota_add_fusion.5, f32[]{:T(128)} %get-tuple-element.478, bf16[2048,1152]{1,0:T(8,128)(2,1)} %get-tuple-element.477, bf16[128,1152]{1,0:T(8,128)(2,1)S(1)} %copy.15, f32[]{:T(128)} %get-tuple-element.476), kind=kOutput, calls=%fused_computation.16.clone.1 | convolution fusion | flops 607387648 | bytes 6070796 | tf_op jit(solution)/shard_map/while/body/eval_jaxpr/dot_general | solution.py:46
  207.4 6.8 %convolution_add_fusion.5 = f32[2048,1152]{1,0:T(8,128)} fusion(bf16[128,1152]{1,0:T(8,128)(2,1)S(1)} %copy.15, f32[2048,1152]{1,0:T(8,128)} %get-tuple-element.455, pred[]{:T(512)S(6)} %compare.9, f32[2048,128]{1,0:T(8,128)S(1)} %get-tuple-element.433, s32[128]{0:T(128)S(1)} %iota_add_fusion.4, s32[2048]{0:T(1024)S(1)} %iota_add_fusion.5), kind=kOutput, calls=%fused_computation.2.clone.1 | convolution fusion | flops 611057664 | bytes 20226560 | tf_op jit(solution)/shard_map/while/body/eval_jaxpr/dot_general | solution.py:54
  220.3 5.3 %all-to-all-start.1 = ((f32[16,16,1152]{2,1,0:T(8,128)}), f32[16,16,1152]{2,1,0:T(8,128)S(1)}, u32[]{:S(2)}, u32[]{:S(2)}) async-start(f32[16,16,1152]{2,1,0:T(8,128)} %bitcast.4), calls=%async_computation.2 | async-start | bytes 2359296 | tf_op jit(solution)/shard_map/all_to_all | solution.py:125
  225.6 9.2 %psum.28 = f32[]{:T(128)} all-reduce(f32[]{:T(128)} %get-tuple-element.294), channel_id=1, replica_groups=mesh['group_0'=4,'group_1'=2,'dev_0'=4,'dev_1'=4] {'group_0'}, use_global_device_ids=true, to_apply=%region_10.11 | all-reduce | flops 1 | bytes 8 | tf_op jit(solution)/shard_map/psum | solution.py:22
  234.7 3.1 psum.29
  237.8 11.5 %psum.30 = f32[]{:T(128)} all-reduce(f32[]{:T(128)} %psum.29), channel_id=1, replica_groups=mesh['group_0'=4,'group_1'=2,'dev_0'=4,'dev_1'=4] {'dev_0'}, use_global_device_ids=true, to_apply=%region_12.13 | all-reduce | flops 1 | bytes 8 | tf_op jit(solution)/shard_map/psum | solution.py:22
  249.3 11.1 %psum.31 = f32[]{:T(128)} all-reduce(f32[]{:T(128)} %psum.30), channel_id=1, replica_groups=mesh['group_0'=4,'group_1'=2,'dev_0'=4,'dev_1'=4] {'dev_1'}, use_global_device_ids=true, to_apply=%region_13.14 | all-reduce | flops 1 | bytes 8 | tf_op jit(solution)/shard_map/psum | solution.py:22
  262.8 50.6 %reduce-scatter.2.cloned.1.call-done = f32[128,1152]{1,0:T(8,128)} async-done(((f32[2048,1152]{1,0:T(8,128)}), f32[128,1152]{1,0:T(8,128)}) %reduce-scatter.2.cloned.1.call-update) | async-done | bytes 589840 | tf_op jit(solution)/shard_map/reduce_scatter | solution.py:113
  (103 shorter events, 35.6 us)
Async XLA Ops:
  7.2 63.9 %all-gather.2.cloned.1.call-start = ((), (), s32[]{:S(2)}) async-start(), calls=%async_computation.3 | async-start | bytes 5013504 | tf_op jit(solution)/shard_map/all_gather | solution.py:90
  14.9 23.3 %all-to-all-start = ((bf16[16,16,1152]{2,1,0:T(8,128)(2,1)}), bf16[16,16,1152]{2,1,0:T(8,128)(2,1)S(1)}, u32[]{:S(2)}, u32[]{:S(2)}) async-start(bf16[16,16,1152]{2,1,0:T(8,128)(2,1)} %bitcast.1), calls=%async_computation | async-start | bytes 1179648 | tf_op jit(solution)/shard_map/all_to_all | solution.py:81
  23.1 290.4 %reduce-scatter.2.cloned.1.call-start = ((), (), s32[]{:S(2)}) async-start(), calls=%async_computation.4 | async-start | bytes 10027008 | tf_op jit(solution)/shard_map/reduce_scatter | solution.py:113
  71.2 14.4 %collective-permute-start = (bf16[128,1152]{1,0:T(8,128)(2,1)S(1)}, bf16[128,1152]{1,0:T(8,128)(2,1)S(1)}, u32[]{:S(2)}, u32[]{:S(2)}) collective-permute-start(bf16[128,1152]{1,0:T(8,128)(2,1)S(1)} %copy.15), channel_id=1, source_target_pairs={{0,16},{16,32},{32,48},{48,64},{64,80},{80,96},{96,112},{112,0},{1... | collective-permute-start | bytes 884744 | tf_op jit(solution)/shard_map/while/body/eval_jaxpr/ppermute | solution.py:17
  71.2 6.3 %copy-start.2 = (bf16[2048,1152]{1,0:T(8,128)(2,1)S(1)}, bf16[2048,1152]{1,0:T(8,128)(2,1)}, u32[]{:S(2)}) copy-start(bf16[2048,1152]{1,0:T(8,128)(2,1)} %get-tuple-element.477) | copy-start | bytes 14155780 | tf_op jit(solution)/shard_map/while
  78.9 10.5 %collective-permute-start.1 = (f32[128,1152]{1,0:T(8,128)S(1)}, f32[128,1152]{1,0:T(8,128)S(1)}, u32[]{:S(2)}, u32[]{:S(2)}) collective-permute-start(f32[128,1152]{1,0:T(8,128)S(1)} %convolution_add_fusion.4), channel_id=1, source_target_pairs={{0,16},{16,32},{32,48},{48,64},{64,80},{80,96},{96,112},{112,0},{1... | collective-permute-start | bytes 1769480 | tf_op jit(solution)/shard_map/while/body/eval_jaxpr/ppermute | solution.py:17
  89.5 15.6 %collective-permute-start = (bf16[128,1152]{1,0:T(8,128)(2,1)S(1)}, bf16[128,1152]{1,0:T(8,128)(2,1)S(1)}, u32[]{:S(2)}, u32[]{:S(2)}) collective-permute-start(bf16[128,1152]{1,0:T(8,128)(2,1)S(1)} %copy.15), channel_id=1, source_target_pairs={{0,16},{16,32},{32,48},{48,64},{64,80},{80,96},{96,112},{112,0},{1... | collective-permute-start | bytes 884744 | tf_op jit(solution)/shard_map/while/body/eval_jaxpr/ppermute | solution.py:17
  89.6 6.3 %copy-start.2 = (bf16[2048,1152]{1,0:T(8,128)(2,1)S(1)}, bf16[2048,1152]{1,0:T(8,128)(2,1)}, u32[]{:S(2)}) copy-start(bf16[2048,1152]{1,0:T(8,128)(2,1)} %get-tuple-element.477) | copy-start | bytes 14155780 | tf_op jit(solution)/shard_map/while
  97.3 10.5 %collective-permute-start.1 = (f32[128,1152]{1,0:T(8,128)S(1)}, f32[128,1152]{1,0:T(8,128)S(1)}, u32[]{:S(2)}, u32[]{:S(2)}) collective-permute-start(f32[128,1152]{1,0:T(8,128)S(1)} %convolution_add_fusion.4), channel_id=1, source_target_pairs={{0,16},{16,32},{32,48},{48,64},{64,80},{80,96},{96,112},{112,0},{1... | collective-permute-start | bytes 1769480 | tf_op jit(solution)/shard_map/while/body/eval_jaxpr/ppermute | solution.py:17
  107.8 15.3 %collective-permute-start = (bf16[128,1152]{1,0:T(8,128)(2,1)S(1)}, bf16[128,1152]{1,0:T(8,128)(2,1)S(1)}, u32[]{:S(2)}, u32[]{:S(2)}) collective-permute-start(bf16[128,1152]{1,0:T(8,128)(2,1)S(1)} %copy.15), channel_id=1, source_target_pairs={{0,16},{16,32},{32,48},{48,64},{64,80},{80,96},{96,112},{112,0},{1... | collective-permute-start | bytes 884744 | tf_op jit(solution)/shard_map/while/body/eval_jaxpr/ppermute | solution.py:17
  107.9 6.3 %copy-start.2 = (bf16[2048,1152]{1,0:T(8,128)(2,1)S(1)}, bf16[2048,1152]{1,0:T(8,128)(2,1)}, u32[]{:S(2)}) copy-start(bf16[2048,1152]{1,0:T(8,128)(2,1)} %get-tuple-element.477) | copy-start | bytes 14155780 | tf_op jit(solution)/shard_map/while
  115.6 10.5 %collective-permute-start.1 = (f32[128,1152]{1,0:T(8,128)S(1)}, f32[128,1152]{1,0:T(8,128)S(1)}, u32[]{:S(2)}, u32[]{:S(2)}) collective-permute-start(f32[128,1152]{1,0:T(8,128)S(1)} %convolution_add_fusion.4), channel_id=1, source_target_pairs={{0,16},{16,32},{32,48},{48,64},{64,80},{80,96},{96,112},{112,0},{1... | collective-permute-start | bytes 1769480 | tf_op jit(solution)/shard_map/while/body/eval_jaxpr/ppermute | solution.py:17
  126.2 15.3 %collective-permute-start = (bf16[128,1152]{1,0:T(8,128)(2,1)S(1)}, bf16[128,1152]{1,0:T(8,128)(2,1)S(1)}, u32[]{:S(2)}, u32[]{:S(2)}) collective-permute-start(bf16[128,1152]{1,0:T(8,128)(2,1)S(1)} %copy.15), channel_id=1, source_target_pairs={{0,16},{16,32},{32,48},{48,64},{64,80},{80,96},{96,112},{112,0},{1... | collective-permute-start | bytes 884744 | tf_op jit(solution)/shard_map/while/body/eval_jaxpr/ppermute | solution.py:17
  126.3 6.3 %copy-start.2 = (bf16[2048,1152]{1,0:T(8,128)(2,1)S(1)}, bf16[2048,1152]{1,0:T(8,128)(2,1)}, u32[]{:S(2)}) copy-start(bf16[2048,1152]{1,0:T(8,128)(2,1)} %get-tuple-element.477) | copy-start | bytes 14155780 | tf_op jit(solution)/shard_map/while
  134.0 10.5 %collective-permute-start.1 = (f32[128,1152]{1,0:T(8,128)S(1)}, f32[128,1152]{1,0:T(8,128)S(1)}, u32[]{:S(2)}, u32[]{:S(2)}) collective-permute-start(f32[128,1152]{1,0:T(8,128)S(1)} %convolution_add_fusion.4), channel_id=1, source_target_pairs={{0,16},{16,32},{32,48},{48,64},{64,80},{80,96},{96,112},{112,0},{1... | collective-permute-start | bytes 1769480 | tf_op jit(solution)/shard_map/while/body/eval_jaxpr/ppermute | solution.py:17
  144.5 15.3 %collective-permute-start = (bf16[128,1152]{1,0:T(8,128)(2,1)S(1)}, bf16[128,1152]{1,0:T(8,128)(2,1)S(1)}, u32[]{:S(2)}, u32[]{:S(2)}) collective-permute-start(bf16[128,1152]{1,0:T(8,128)(2,1)S(1)} %copy.15), channel_id=1, source_target_pairs={{0,16},{16,32},{32,48},{48,64},{64,80},{80,96},{96,112},{112,0},{1... | collective-permute-start | bytes 884744 | tf_op jit(solution)/shard_map/while/body/eval_jaxpr/ppermute | solution.py:17
  144.6 6.3 %copy-start.2 = (bf16[2048,1152]{1,0:T(8,128)(2,1)S(1)}, bf16[2048,1152]{1,0:T(8,128)(2,1)}, u32[]{:S(2)}) copy-start(bf16[2048,1152]{1,0:T(8,128)(2,1)} %get-tuple-element.477) | copy-start | bytes 14155780 | tf_op jit(solution)/shard_map/while
  152.3 10.5 %collective-permute-start.1 = (f32[128,1152]{1,0:T(8,128)S(1)}, f32[128,1152]{1,0:T(8,128)S(1)}, u32[]{:S(2)}, u32[]{:S(2)}) collective-permute-start(f32[128,1152]{1,0:T(8,128)S(1)} %convolution_add_fusion.4), channel_id=1, source_target_pairs={{0,16},{16,32},{32,48},{48,64},{64,80},{80,96},{96,112},{112,0},{1... | collective-permute-start | bytes 1769480 | tf_op jit(solution)/shard_map/while/body/eval_jaxpr/ppermute | solution.py:17
  162.9 15.3 %collective-permute-start = (bf16[128,1152]{1,0:T(8,128)(2,1)S(1)}, bf16[128,1152]{1,0:T(8,128)(2,1)S(1)}, u32[]{:S(2)}, u32[]{:S(2)}) collective-permute-start(bf16[128,1152]{1,0:T(8,128)(2,1)S(1)} %copy.15), channel_id=1, source_target_pairs={{0,16},{16,32},{32,48},{48,64},{64,80},{80,96},{96,112},{112,0},{1... | collective-permute-start | bytes 884744 | tf_op jit(solution)/shard_map/while/body/eval_jaxpr/ppermute | solution.py:17
  162.9 6.3 %copy-start.2 = (bf16[2048,1152]{1,0:T(8,128)(2,1)S(1)}, bf16[2048,1152]{1,0:T(8,128)(2,1)}, u32[]{:S(2)}) copy-start(bf16[2048,1152]{1,0:T(8,128)(2,1)} %get-tuple-element.477) | copy-start | bytes 14155780 | tf_op jit(solution)/shard_map/while
  170.6 10.5 %collective-permute-start.1 = (f32[128,1152]{1,0:T(8,128)S(1)}, f32[128,1152]{1,0:T(8,128)S(1)}, u32[]{:S(2)}, u32[]{:S(2)}) collective-permute-start(f32[128,1152]{1,0:T(8,128)S(1)} %convolution_add_fusion.4), channel_id=1, source_target_pairs={{0,16},{16,32},{32,48},{48,64},{64,80},{80,96},{96,112},{112,0},{1... | collective-permute-start | bytes 1769480 | tf_op jit(solution)/shard_map/while/body/eval_jaxpr/ppermute | solution.py:17
  181.2 15.3 %collective-permute-start = (bf16[128,1152]{1,0:T(8,128)(2,1)S(1)}, bf16[128,1152]{1,0:T(8,128)(2,1)S(1)}, u32[]{:S(2)}, u32[]{:S(2)}) collective-permute-start(bf16[128,1152]{1,0:T(8,128)(2,1)S(1)} %copy.15), channel_id=1, source_target_pairs={{0,16},{16,32},{32,48},{48,64},{64,80},{80,96},{96,112},{112,0},{1... | collective-permute-start | bytes 884744 | tf_op jit(solution)/shard_map/while/body/eval_jaxpr/ppermute | solution.py:17
  181.3 6.3 %copy-start.2 = (bf16[2048,1152]{1,0:T(8,128)(2,1)S(1)}, bf16[2048,1152]{1,0:T(8,128)(2,1)}, u32[]{:S(2)}) copy-start(bf16[2048,1152]{1,0:T(8,128)(2,1)} %get-tuple-element.477) | copy-start | bytes 14155780 | tf_op jit(solution)/shard_map/while
  189.0 10.5 %collective-permute-start.1 = (f32[128,1152]{1,0:T(8,128)S(1)}, f32[128,1152]{1,0:T(8,128)S(1)}, u32[]{:S(2)}, u32[]{:S(2)}) collective-permute-start(f32[128,1152]{1,0:T(8,128)S(1)} %convolution_add_fusion.4), channel_id=1, source_target_pairs={{0,16},{16,32},{32,48},{48,64},{64,80},{80,96},{96,112},{112,0},{1... | collective-permute-start | bytes 1769480 | tf_op jit(solution)/shard_map/while/body/eval_jaxpr/ppermute | solution.py:17
  199.5 15.3 %collective-permute-start = (bf16[128,1152]{1,0:T(8,128)(2,1)S(1)}, bf16[128,1152]{1,0:T(8,128)(2,1)S(1)}, u32[]{:S(2)}, u32[]{:S(2)}) collective-permute-start(bf16[128,1152]{1,0:T(8,128)(2,1)S(1)} %copy.15), channel_id=1, source_target_pairs={{0,16},{16,32},{32,48},{48,64},{64,80},{80,96},{96,112},{112,0},{1... | collective-permute-start | bytes 884744 | tf_op jit(solution)/shard_map/while/body/eval_jaxpr/ppermute | solution.py:17
  199.6 6.3 %copy-start.2 = (bf16[2048,1152]{1,0:T(8,128)(2,1)S(1)}, bf16[2048,1152]{1,0:T(8,128)(2,1)}, u32[]{:S(2)}) copy-start(bf16[2048,1152]{1,0:T(8,128)(2,1)} %get-tuple-element.477) | copy-start | bytes 14155780 | tf_op jit(solution)/shard_map/while
  207.3 10.5 %collective-permute-start.1 = (f32[128,1152]{1,0:T(8,128)S(1)}, f32[128,1152]{1,0:T(8,128)S(1)}, u32[]{:S(2)}, u32[]{:S(2)}) collective-permute-start(f32[128,1152]{1,0:T(8,128)S(1)} %convolution_add_fusion.4), channel_id=1, source_target_pairs={{0,16},{16,32},{32,48},{48,64},{64,80},{80,96},{96,112},{112,0},{1... | collective-permute-start | bytes 1769480 | tf_op jit(solution)/shard_map/while/body/eval_jaxpr/ppermute | solution.py:17
  217.9 43.2 %copy-start = (bf16[128,1152]{1,0:T(8,128)(2,1)S(1)}, bf16[128,1152]{1,0:T(8,128)(2,1)}, u32[]{:S(2)}) copy-start(bf16[128,1152]{1,0:T(8,128)(2,1)} %param.9) | copy-start | bytes 884740
  217.9 95.6 %copy-start.1 = (bf16[128,1152]{1,0:T(8,128)(2,1)S(1)}, bf16[128,1152]{1,0:T(8,128)(2,1)}, u32[]{:S(2)}) copy-start(bf16[128,1152]{1,0:T(8,128)(2,1)} %param.8) | copy-start | bytes 884740
  220.3 40.8 %all-to-all-start.1 = ((f32[16,16,1152]{2,1,0:T(8,128)}), f32[16,16,1152]{2,1,0:T(8,128)S(1)}, u32[]{:S(2)}, u32[]{:S(2)}) async-start(f32[16,16,1152]{2,1,0:T(8,128)} %bitcast.4), calls=%async_computation.2 | async-start | bytes 2359296 | tf_op jit(solution)/shard_map/all_to_all | solution.py:125
Sparse Core Ops, SparseCore 0:
  10.7 60.2 all-gather.1
  218.0 95.3 reduce-scatter.1
where the time goes:
time: 326 us; the launch traced here: 325 us
  waiting for transfers between devices  122 us (37%)
  matrix products  119 us (37%)
  blocking collectives  34.8 us (11%)
  between operations  16.6 us (5%)
  starting transfers between devices  15.6 us (5%)
  other arithmetic  10.9 us (3%)
  loops' own time  5.89 us (2%)
    dot_general x8, matrix products, block_terms(): dimg_part = jnp.dot(coeff, stretch, preferred_element_type=jnp.float32)  52.3 us
    reduce_scatter x1, waiting for transfers between devices, per_device(): dimg_own = lax.psum_scatter(dimg_acc, DEV, scatter_dimension=0, tiled=True)  50.6 us
    dot_general x8, matrix products, block_terms(): lax.dot_general(img_block, stretch, (((1,), (1,)), ((), ())), preferred_e...  49.9 us
    psum x4, blocking collectives, over_axes(): array = lax.psum(array, axis)  34.8 us
    all_gather x1, waiting for transfers between devices, per_device(): img_block = lax.all_gather(img_half, DEV, axis=0, tiled=True)  32.6 us
    ppermute x16, waiting for transfers between devices, from_behind(): lax.ppermute(array, axis, [(i, (i + by) % count) for i in range(count)])  24.7 us
    all_to_all x1, waiting for transfers between devices, per_device(): lax.all_to_all(outgoing, DEV, split_axis=0, concat_axis=0, tiled=True)  14.2 us
    dot_general x8, matrix products, block_terms(): lax.dot_general(coeff, img_block, (((0,), (0,)), ((), ())), preferred_ele...  11.6 us
  transfers between devices with their start and end apart: 20, of which 11 were waited for; matrix products, arithmetic and copies ran while one was open for 38% of the time, Pallas kernels for 0%

commit v1 on v0

v1 whole, which is shorter than its diff:
```python
import jax
import jax.numpy as jnp
from jax import lax
from jax.sharding import Mesh
from jax.sharding import PartitionSpec as P

DEV = ("dev_0", "dev_1")
GROUP = ("group_0", "group_1")
GROUP_DEV = ("group_0", "group_1", "dev_0", "dev_1")


EPSILON = 1e-06


def normalize(values):
    wide = values.astype(jnp.float32)
    recip = lax.rsqrt(jnp.sum(wide * wide, axis=1, keepdims=True) + EPSILON)
    return (wide * recip, recip)


def project_back(unit, recip, grad):
    return recip * (grad - unit * jnp.sum(unit * grad, axis=1, keepdims=True))


def per_device(images, texts, lang_order, position, logit_scale, logit_bias):
    row_count, width_count = images.shape
    dev_count = lax.axis_size(DEV)
    group_count = lax.axis_size(GROUP)
    scale = logit_scale[0]
    bias = logit_bias[0]
    span = row_count * dev_count
    group_index = lax.axis_index(GROUP)
    img_unit, img_recip = normalize(images)
    txt_unit, txt_recip = normalize(texts)
    img_block = lax.all_gather(img_unit.astype(jnp.bfloat16), DEV, axis=0, tiled=True)
    txt_block = lax.all_gather(txt_unit.astype(jnp.bfloat16), GROUP, axis=0, tiled=True)
    txt_ids = lax.all_gather(group_index * span + lang_order, GROUP, axis=0, tiled=True)
    img_ids = group_index * span + jnp.arange(span, dtype=jnp.int32)
    logits = (
        scale
        * lax.dot_general(
            img_block, txt_block, (((1,), (1,)), ((), ())), preferred_element_type=jnp.float32
        )
        + bias
    )
    sign = jnp.where(img_ids[:, None] == txt_ids[None, :], jnp.float32(1.0), jnp.float32(-1.0))
    loss_part = jnp.sum(-jax.nn.log_sigmoid(sign * logits))
    coeff = (-sign * jax.nn.sigmoid(-sign * logits)).astype(jnp.bfloat16)
    dimg_part = jnp.dot(coeff, txt_block, preferred_element_type=jnp.float32)
    dtext_part = lax.dot_general(
        coeff, img_block, (((0,), (0,)), ((), ())), preferred_element_type=jnp.float32
    )
    dimg = scale * lax.psum_scatter(dimg_part, DEV, scatter_dimension=0, tiled=True)
    dtext = scale * lax.psum_scatter(dtext_part, GROUP, scatter_dimension=0, tiled=True)
    total = jnp.float32(span * group_count)
    loss = (lax.psum(loss_part, GROUP_DEV) / (total * total)).reshape(1)
    return (
        project_back(img_unit, img_recip, dimg),
        project_back(txt_unit, txt_recip, dtext),
        loss,
    )


def solution(mesh):
    finer = Mesh(mesh.devices.reshape(4, 2, 4, 4), GROUP_DEV)
    return jax.shard_map(
        per_device,
        mesh=finer,
        in_specs=(P(GROUP_DEV, None), P(GROUP_DEV, None), P(GROUP_DEV), P(GROUP_DEV), P(), P()),
        out_specs=(P(GROUP_DEV, None), P(GROUP_DEV, None), P()),
        check_vma=False,
    )
```

time: 326 us -> 263 us (0.81)
  matrix products: 119 us -> 33.5 us
  blocking collectives: 34.8 us -> 76.5 us
  starting transfers between devices: 15.6 us -> 0.16 us
  loops' own time: 5.89 us -> 0 us
    dot_general x28 -> x3, matrix products: 119 us -> 33.5 us  [the longest x1 16.4 us: per_device(): lax.dot_general(img_block, txt_block, (((1,), (1,)), ((), ())), preferred...]
    all_gather x1 -> x2, waiting for transfers between devices: 32.6 us -> 69.8 us  [the longest x1 57.3 us: per_device(): lax.all_gather(img_unit.astype(jnp.bfloat16), DEV, axis=0, tiled=True)]
    psum x4 -> x1, blocking collectives: 34.8 us -> 65.9 us  [per_device(): loss = (lax.psum(loss_part, GROUP_DEV) / (total * total)).reshape(1)]
    ppermute x16 -> x0, waiting for transfers between devices: 24.7 us -> none  [from_behind(): lax.ppermute(array, axis, [(i, (i + by) % count) for i in range(count)])]
    all_to_all x2 -> x0, waiting for transfers between devices: 14.2 us -> none  [the longest x1 14.2 us: per_device(): lax.all_to_all(outgoing, DEV, split_axis=0, concat_axis=0, tiled=True)]
    all_to_all x2 -> x0, starting transfers between devices: 13.4 us -> none  [the longest x1 8.16 us: per_device(): lax.all_to_all(outgoing, DEV, split_axis=0, concat_axis=0, tiled=True)]
    all_gather x0 -> x1, blocking collectives: none -> 10.6 us  [per_device(): lax.all_gather(group_index * span + lang_order, GROUP, axis=0, tiled=True)]
    another operation x1 -> x0, loops' own time: 5.89 us -> none  [per_device(): lax.fori_loop(0, group_count, turn_group, init)]
  transfers between devices with their start and end apart: 20 -> 4, of which waited for: 11 -> 3; matrix products, arithmetic and copies ran while one was open for 38% -> 6% of each run, Pallas kernels for 0% -> 0%
where the time goes in v1:
time: 263 us
  waiting for transfers between devices  121 us (46%)
  blocking collectives  76.5 us (29%)
  matrix products  33.5 us (13%)
  between operations  16.9 us (6%)
  other arithmetic  13.3 us (5%)
    psum x1, blocking collectives, per_device(): loss = (lax.psum(loss_part, GROUP_DEV) / (total * total)).reshape(1)  65.9 us
    all_gather x1, waiting for transfers between devices, per_device(): lax.all_gather(img_unit.astype(jnp.bfloat16), DEV, axis=0, tiled=True)  57.3 us
    reduce_scatter x1, waiting for transfers between devices, per_device(): lax.psum_scatter(dimg_part, DEV, scatter_dimension=0, tiled=True)  50.7 us
    dot_general x1, matrix products, per_device(): lax.dot_general(img_block, txt_block, (((1,), (1,)), ((), ())), preferred...  16.4 us
    all_gather x1, waiting for transfers between devices, per_device(): lax.all_gather(txt_unit.astype(jnp.bfloat16), GROUP, axis=0, tiled=True)  12.5 us
    all_gather x1, blocking collectives, per_device(): lax.all_gather(group_index * span + lang_order, GROUP, axis=0, tiled=True)  10.6 us
    dot_general x1, matrix products, per_device(): dimg_part = jnp.dot(coeff, txt_block, preferred_element_type=jnp.float32)  9.57 us
    dot_general x1, matrix products, per_device(): lax.dot_general(coeff, img_block, (((0,), (0,)), ((), ())), preferred_ele...  7.55 us
  transfers between devices with their start and end apart: 4, of which 3 were waited for; matrix products, arithmetic and copies ran while one was open for 6% of the time, Pallas kernels for 0%

profile of v1, /device:TPU:0, one launch (start us, length us, event | category | flops | bytes accessed | tf_op | source)
XLA Modules:
  0.0 262.9 jit_solution(11099517485220100941)
XLA Ops:
  7.2 0.0 all-gather.6.cloned.1.call-start
  7.2 1.1 fusion.22
  8.3 1.8 fusion.11
  10.1 0.0 all-gather.6.cloned.1.call-update
  10.1 0.0 all-gather.4.cloned.1.call-start
  10.2 1.1 fusion.18
  11.3 1.8 fusion.14
  13.1 0.0 all-gather.4.cloned.1.call-update
  13.1 0.0 reduce-scatter.5.cloned.1.call-start
  14.5 0.7 add_bitcast_fusion
  15.1 10.6 %all-gather = s32[8,1,128]{2,1,0:T(1,128)S(1)} all-gather(s32[1,1,128]{2,1,0:T(1,128)S(1)} %add_bitcast_fusion), channel_id=1, replica_groups=mesh['group_0'=4,'group_1'=2,'dev_0'=4,'dev_1'=4] {'group_0','group_1'}, dimensions={0}, use_global_device_ids=true | all-gather | bytes 4608 | tf_op jit(solution)/shard_map/all_gather | solution.py:37
  25.8 12.5 %all-gather.6.cloned.1.call-done = bf16[1024,1152]{1,0:T(8,128)(2,1)} async-done(((bf16[128,1152]{1,0:T(8,128)(2,1)}), bf16[1024,1152]{1,0:T(8,128)(2,1)}) %all-gather.6.cloned.1.call-update) | async-done | bytes 2359312 | tf_op jit(solution)/shard_map/all_gather | solution.py:36
  38.3 57.3 %all-gather.4.cloned.1.call-done = bf16[2048,1152]{1,0:T(8,128)(2,1)} async-done(((bf16[128,1152]{1,0:T(8,128)(2,1)}), bf16[2048,1152]{1,0:T(8,128)(2,1)}) %all-gather.4.cloned.1.call-update) | async-done | bytes 4718608 | tf_op jit(solution)/shard_map/all_gather | solution.py:35
  95.6 0.0 copy-start.2
  95.6 16.4 %fusion.7 = (f32[]{:T(128)}, bf16[2048,1024]{1,0:T(8,128)(2,1)S(1)}) fusion(f32[]{:T(128)} %bitcast.17, f32[]{:T(128)} %bitcast.14, s32[1024]{0:T(1024)S(1)} %bitcast.18, s32[2048]{0:T(1024)S(1)} %iota_add_fusion, bf16[2048,1152]{1,0:T(8,128)(2,1)} %all-gather.4.cloned.1.call-done, bf16[1024,1152]{1,0:T(8,128)(2,1)} %all-gather.6.cloned.1.call-done), kind=kOutput, calls=%fused_computation.10 | convolution fusion | flops 4873781248 | bytes 11284492 | tf_op jit(solution)/shard_map/dot_general | solution.py:41
  112.0 1.9 copy-done.4
  113.9 0.0 copy-done.2
  113.9 7.6 %fusion.24 = f32[1024,1152]{1,0:T(8,128)} fusion(bf16[2048,1024]{1,0:T(8,128)(2,1)S(1)} %get-tuple-element.4, bf16[2048,1152]{1,0:T(8,128)(2,1)S(1)} %copy-done.2), kind=kOutput, calls=%fused_computation.36 | convolution fusion | flops 4831838208 | bytes 13631488 | tf_op jit(solution)/shard_map/dot_general | solution.py:50
  121.5 0.0 reduce-scatter.5.cloned.1.call-update
  121.5 0.0 reduce-scatter.3.cloned.1.call-start
  121.6 0.0 copy-done.3
  121.6 9.6 %fusion.23 = f32[2048,1152]{1,0:T(8,128)} fusion(bf16[2048,1024]{1,0:T(8,128)(2,1)} %copy-done.4, bf16[1024,1152]{1,0:T(8,128)(2,1)S(1)} %copy-done.3), kind=kOutput, calls=%fused_computation.35 | convolution fusion | flops 4831838208 | bytes 15990784 | tf_op jit(solution)/shard_map/dot_general | solution.py:49
  131.2 0.0 reduce-scatter.3.cloned.1.call-update
  131.2 65.9 %psum.7 = f32[]{:T(128)} all-reduce(f32[]{:T(128)} %get-tuple-element.3), channel_id=1, replica_groups=mesh['group_0'=4,'group_1'=2,'dev_0'=4,'dev_1'=4] {'group_0','group_1','..., use_global_device_ids=true, to_apply=%region_7.8 | all-reduce | flops 1 | bytes 8 | tf_op jit(solution)/shard_map/psum | solution.py:56
  197.7 0.0 reduce-scatter.5.cloned.1.call-done
  197.7 0.0 copy-done
  197.8 1.3 fusion.19
  199.1 2.1 fusion.21
  201.2 50.7 %reduce-scatter.3.cloned.1.call-done = f32[128,1152]{1,0:T(8,128)} async-done(((f32[2048,1152]{1,0:T(8,128)}), f32[128,1152]{1,0:T(8,128)}) %reduce-scatter.3.cloned.1.call-update) | async-done | bytes 589840 | tf_op jit(solution)/shard_map/reduce_scatter | solution.py:53
  251.8 0.0 copy-done.1
  251.8 1.3 fusion.15
  253.1 2.1 fusion.17
  (7 shorter events, 0.0 us)
Async XLA Ops:
  7.2 31.2 %all-gather.6.cloned.1.call-start = ((), (), s32[]{:S(2)}) async-start(), calls=%async_computation.3 | async-start | bytes 2654208 | tf_op jit(solution)/shard_map/all_gather | solution.py:36
  10.1 85.5 %all-gather.4.cloned.1.call-start = ((), (), s32[]{:S(2)}) async-start(), calls=%async_computation.2 | async-start | bytes 5013504 | tf_op jit(solution)/shard_map/all_gather | solution.py:35
  13.1 184.6 %reduce-scatter.5.cloned.1.call-start = ((), (), s32[]{:S(2)}) async-start(), calls=%async_computation.5 | async-start | bytes 5308416 | tf_op jit(solution)/shard_map/reduce_scatter | solution.py:54
  95.6 18.3 %copy-start.2 = (bf16[2048,1152]{1,0:T(8,128)(2,1)S(1)}, bf16[2048,1152]{1,0:T(8,128)(2,1)}, u32[]{:S(2)}) copy-start(bf16[2048,1152]{1,0:T(8,128)(2,1)} %all-gather.4.cloned.1.call-done) | copy-start | bytes 14155780
  112.0 1.9 copy-start.4
  113.9 7.6 %copy-start.3 = (bf16[1024,1152]{1,0:T(8,128)(2,1)S(1)}, bf16[1024,1152]{1,0:T(8,128)(2,1)}, u32[]{:S(2)}) copy-start(bf16[1024,1152]{1,0:T(8,128)(2,1)} %all-gather.6.cloned.1.call-done) | copy-start | bytes 7077892
  121.5 130.3 %reduce-scatter.3.cloned.1.call-start = ((), (), s32[]{:S(2)}) async-start(), calls=%async_computation.4 | async-start | bytes 10027008 | tf_op jit(solution)/shard_map/reduce_scatter | solution.py:53
  131.1 66.6 %copy-start = (bf16[128,1152]{1,0:T(8,128)(2,1)S(1)}, bf16[128,1152]{1,0:T(8,128)(2,1)}, u32[]{:S(2)}) copy-start(bf16[128,1152]{1,0:T(8,128)(2,1)} %param.7) | copy-start | bytes 884740
  131.1 120.7 %copy-start.1 = (bf16[128,1152]{1,0:T(8,128)(2,1)S(1)}, bf16[128,1152]{1,0:T(8,128)(2,1)}, u32[]{:S(2)}) copy-start(bf16[128,1152]{1,0:T(8,128)(2,1)} %param.6) | copy-start | bytes 884740
Sparse Core Ops, SparseCore 0:
  10.3 28.0 all-gather.5
  41.1 54.4 all-gather.3
  121.6 39.0 reduce-scatter.4
  164.1 87.6 reduce-scatter.2

commit v2 on v1

v2 whole, which is shorter than its diff:
```python
import jax
import jax.numpy as jnp
from jax import lax
from jax.experimental import pallas as pl
from jax.experimental.pallas import tpu as pltpu
from jax.sharding import Mesh
from jax.sharding import PartitionSpec as P

AXES = ("x", "core", "y", "z")
MESH = pl.DeviceIdType.MESH
EPSILON = 1e-06
ROWS = 128
BF16 = jnp.bfloat16
F32 = jnp.float32

PLACES = ((0, 0), (0, 1), (1, 0), (3, 0), (1, 1), (3, 1), (2, 0), (2, 1))
AT = {place: index for index, place in enumerate(PLACES)}
N_PLACE = len(PLACES)

GATHER = ("z", "plus_own", "minus_own", "plus_par", "minus_par", "plus_far", "minus_far")
REDUCE = ("far_plus", "far_minus", "near_plus", "near_minus", "relay_plus", "relay_minus", "z")
FLOWS = {}
for kind in ("img", "txt", "ids"):
    for name in GATHER:
        FLOWS[kind, name] = len(FLOWS)
for kind in ("dimg", "dimg_s", "dtxt", "dtxt_s"):
    for name in REDUCE:
        FLOWS[kind, name] = len(FLOWS)
for place in range(N_PLACE):
    FLOWS["share", place] = len(FLOWS)
for place in range(N_PLACE):
    FLOWS["swap", place] = len(FLOWS)
FLOWS["loss_core"] = len(FLOWS)
for axis in ("x", "y", "z"):
    for step in (1, 2, 3):
        FLOWS["loss", axis, step] = len(FLOWS)
N_FLOW = len(FLOWS)


def normalize(values):
    wide = values.astype(F32)
    recip = lax.rsqrt(jnp.sum(wide * wide, axis=1, keepdims=True) + EPSILON)
    return (wide * recip, recip)


def project_back(unit, recip, grad):
    return recip * (grad - unit * jnp.sum(unit * grad, axis=1, keepdims=True))


def kernel(
    img_in, txt_in, ids_in, scale_ref, bias_ref,
    img_out, txt_out, loss_out,
    img, txt, ids, dimg, swap, dtxt, coeff, sent, sent_s, got, got_s, loss_tile, loss_got,
    send_sem, recv_sem,
):
    x, core = lax.axis_index("x"), lax.axis_index("core")
    y, z = lax.axis_index("y"), lax.axis_index("z")
    other = {"core": 1 - core}
    z_img = z + 1 - 2 * lax.rem(z, 2)
    z_txt = 3 - z
    plus = {"img": {"x": lax.rem(x + 1, 4)}, "txt": {"y": lax.rem(y + 1, 4)}}
    minus = {"img": {"x": lax.rem(x + 3, 4)}, "txt": {"y": lax.rem(y + 3, 4)}}
    across = {"img": {"z": z_img}, "txt": {"z": z_txt}}

    started = []

    def copy(flow, src, dst, device):
        return pltpu.make_async_remote_copy(
            src_ref=src, dst_ref=dst, send_sem=send_sem.at[flow], recv_sem=recv_sem.at[flow],
            device_id=device, device_id_type=MESH,
        )

    barrier = pltpu.get_barrier_semaphore()
    peers = [other]
    for axis, here in (("x", x), ("y", y), ("z", z)):
        for step in (1, 2, 3):
            peers.append({axis: lax.rem(here + step, 4)})
    for peer in peers:
        pl.semaphore_signal(barrier, inc=1, device_id=peer, device_id_type=MESH)

    def img_rows(place, which):
        return pl.ds((2 * place + which) * ROWS, ROWS)

    def rows(place):
        return pl.ds(place * ROWS, ROWS)

    img[img_rows(0, 0), :] = normalize(img_in[...])[0].astype(BF16)
    txt[rows(0), :] = normalize(txt_in[...])[0].astype(BF16)
    ids[0] = ids_in[...]
    scale = scale_ref[0]
    bias = bias_ref[0]
    dtxt[...] = jnp.zeros_like(dtxt)
    loss_tile[0] = jnp.zeros_like(loss_tile[0])
    pl.semaphore_wait(barrier, len(peers))

    def block(kind, place):
        if kind == "img":
            return img.at[img_rows(place, 0), :]
        if kind == "txt":
            return txt.at[rows(place), :]
        return ids.at[place]

    def gather(kind, name):
        ring = "img" if kind == "img" else "txt"
        src, dst, device = {
            "z": ((0, 0), (0, 1), across[ring]),
            "plus_own": ((0, 0), (3, 0), plus[ring]),
            "minus_own": ((0, 0), (1, 0), minus[ring]),
            "plus_par": ((0, 1), (3, 1), plus[ring]),
            "minus_par": ((0, 1), (1, 1), minus[ring]),
            "plus_far": ((3, 0), (2, 0), plus[ring]),
            "minus_far": ((1, 1), (2, 1), minus[ring]),
        }[name]
        return copy(FLOWS[kind, name], block(kind, AT[src]), block(kind, AT[dst]), device)

    def share(place):
        return copy(
            FLOWS["share", place], img.at[img_rows(place, 0), :], img.at[img_rows(place, 1), :], other
        )

    def go(kind, name):
        descriptor = gather(kind, name)
        descriptor.start()
        started.append(descriptor)
        if kind == "txt":
            go("ids", name)

    def give(place):
        descriptor = share(AT[place])
        descriptor.start()
        started.append(descriptor)

    def come(kind, name):
        gather(kind, name).wait_recv()
        if kind == "txt":
            come("ids", name)

    for name in ("z", "plus_own", "minus_own"):
        go("img", name)
        go("txt", name)
    give((0, 0))
    come("img", "z")
    go("img", "plus_par")
    go("img", "minus_par")
    give((0, 1))
    come("txt", "z")
    go("txt", "plus_par")
    go("txt", "minus_par")
    come("img", "plus_own")
    go("img", "plus_far")
    give((3, 0))
    come("txt", "plus_own")
    go("txt", "plus_far")
    come("img", "minus_own")
    give((1, 0))
    come("txt", "minus_own")
    come("img", "minus_par")
    go("img", "minus_far")
    give((1, 1))
    come("txt", "minus_par")
    go("txt", "minus_far")
    come("img", "plus_par")
    give((3, 1))
    come("txt", "plus_par")
    come("img", "plus_far")
    give((2, 0))
    come("img", "minus_far")
    give((2, 1))
    come("txt", "plus_far")
    come("txt", "minus_far")
    for place in range(N_PLACE):
        share(place).wait_recv()

    row_iota = lax.broadcasted_iota(jnp.int32, (2 * ROWS, 1), 0)

    def give_back(place):
        flow = FLOWS["swap", 0] + place
        return copy(flow, dimg.at[img_rows(place, 1), :], swap.at[rows(place), :], other)

    def step(index, carry):
        place = N_PLACE - 1 - index
        start = pl.multiple_of(place * (2 * ROWS), 2 * ROWS)
        here = img[pl.ds(start, 2 * ROWS), :]
        owner = jnp.where(place == 0, y * 4 + z, y * 4 + z_img) * ROWS
        valid = jnp.logical_and(place < 2, row_iota < ROWS)
        row_ids = jnp.where(valid, owner + row_iota, -1)
        total = jnp.zeros((8, 128), F32)
        for part in range(4):
            columns = pl.ds(part * 256, 256)
            there = txt[columns, :]
            logits = scale * lax.dot_general(
                here, there, (((1,), (1,)), ((), ())), preferred_element_type=F32
            ) + bias
            column_ids = jnp.concatenate([ids[2 * part, 0:1, :], ids[2 * part + 1, 0:1, :]], axis=1)
            same = row_ids == column_ids
            logits = jnp.where(same, -logits, logits)
            small = jnp.exp(-jnp.abs(logits))
            one_plus = 1.0 + small
            recip = 1.0 / one_plus
            sigmoid = jnp.where(logits >= 0, recip, small * recip)
            log1p = jnp.where(
                small < 0.01,
                small * (1.0 - small * (0.5 - small * (1.0 / 3.0))),
                jnp.log(one_plus),
            )
            softplus = jnp.maximum(logits, 0.0) + log1p
            folded = jnp.sum(softplus.reshape(32, 8, 256), axis=0)
            total = total + folded[:, :128] + folded[:, 128:]
            half = jnp.where(same, -sigmoid, sigmoid).astype(BF16)
            coeff[:, columns] = half
            dtxt[columns, :] += lax.dot_general(
                half, here, (((0,), (0,)), ((), ())), preferred_element_type=F32
            )
        dimg[pl.ds(start, 2 * ROWS), :] = jnp.dot(coeff[...], txt[...], preferred_element_type=F32)
        loss_tile[0] += total
        give_back(place).start()
        return carry

    lax.fori_loop(0, N_PLACE, step, 0)

    eye = lax.broadcasted_iota(jnp.int32, (ROWS, ROWS), 0) == lax.broadcasted_iota(
        jnp.int32, (ROWS, ROWS), 1
    )

    def slot(kind, name):
        return REDUCE.index(name) + (0 if kind == "dimg" else len(REDUCE))

    def sum_ref(kind, place):
        if kind == "dimg":
            return dimg.at[img_rows(AT[place], 0), :]
        return dtxt.at[rows(AT[place]), :]

    def route(kind, name):
        ring = "img" if kind == "dimg" else "txt"
        if name == "z":
            return across[ring]
        return plus[ring] if name.endswith("plus") else minus[ring]

    def two(kind, name):
        s = slot(kind, name)
        device = route(kind, name)
        return (
            copy(FLOWS[kind, name], sent.at[s], got.at[s], device),
            copy(FLOWS[kind + "_s", name], sent_s.at[s], got_s.at[s], device),
        )

    def send(kind, name, place):
        ref = sum_ref(kind, place)
        s = slot(kind, name)
        top = jnp.maximum(jnp.max(jnp.abs(ref[...]), axis=1, keepdims=True), 1e-30)
        across_lanes = jnp.sum(jnp.where(eye, top * (1.0 / 32767.0), 0.0), axis=0, keepdims=True)
        sent_s[s] = jnp.broadcast_to(across_lanes, (8, ROWS))
        sent[s] = jnp.round(ref[...] * (32767.0 / top)).astype(jnp.int32).astype(jnp.int16)
        for descriptor in two(kind, name):
            descriptor.start()
            started.append(descriptor)

    def take(kind, name):
        s = slot(kind, name)
        for descriptor in two(kind, name):
            descriptor.wait_recv()
        unit = jnp.sum(jnp.where(eye, got_s[s, 0:1, :], 0.0), axis=1, keepdims=True)
        return got[s].astype(jnp.int32).astype(F32) * unit

    def merge(place):
        give_back(AT[place]).wait_recv()
        dimg[img_rows(AT[place], 0), :] += swap[rows(AT[place]), :]

    for place in ((2, 0), (2, 1), (1, 1), (3, 0), (1, 0), (3, 1), (0, 0), (0, 1)):
        merge(place)
    for name, place in (
        ("far_plus", (2, 0)), ("far_minus", (2, 1)), ("near_plus", (1, 1)), ("near_minus", (3, 0)),
    ):
        for kind in ("dtxt", "dimg"):
            send(kind, name, place)

    loss_copies = []

    def loss_over(axis, here, number):
        loss_got[number, here] = loss_tile[number]
        for stride in (1, 2, 3):
            descriptor = copy(
                FLOWS["loss", axis, stride], loss_tile.at[number], loss_got.at[number, here],
                {axis: lax.rem(here + stride, 4)},
            )
            descriptor.start()
            started.append(descriptor)
        for stride in (1, 2, 3):
            source = lax.rem(here + 4 - stride, 4)
            copy(
                FLOWS["loss", axis, stride], loss_tile.at[number], loss_got.at[number, source],
                {axis: lax.rem(here + stride, 4)},
            ).wait_recv()
        loss_tile[number + 1] = (loss_got[number, 0] + loss_got[number, 1]) + (
            loss_got[number, 2] + loss_got[number, 3]
        )

    descriptor = copy(FLOWS["loss_core"], loss_tile.at[0], loss_got.at[0, 0], other)
    descriptor.start()
    started.append(descriptor)
    descriptor.wait_recv()
    loss_tile[1] = loss_tile[0] + loss_got[0, 0]
    loss_over("x", x, 1)
    loss_over("y", y, 2)
    loss_over("z", z, 3)
    count = F32(ROWS * 128)
    loss_out[0] = jnp.sum(loss_tile[4]) / (count * count)

    for kind in ("dtxt", "dimg"):
        sum_ref(kind, (3, 1))[...] += take(kind, "far_minus")
        send(kind, "relay_minus", (3, 1))
        sum_ref(kind, (1, 0))[...] += take(kind, "far_plus")
        send(kind, "relay_plus", (1, 0))
    for kind in ("dtxt", "dimg"):
        ref = sum_ref(kind, (0, 1))
        ref[...] += take(kind, "near_plus")
        ref[...] += take(kind, "relay_minus")
        send(kind, "z", (0, 1))
    for kind in ("dtxt", "dimg"):
        ref = sum_ref(kind, (0, 0))
        ref[...] += take(kind, "near_minus")
        ref[...] += take(kind, "relay_plus")
    for kind, source, out in (("dtxt", txt_in, txt_out), ("dimg", img_in, img_out)):
        ref = sum_ref(kind, (0, 0))
        ref[...] = scale * (ref[...] + take(kind, "z"))
        unit, recip = normalize(source[...])
        out[...] = project_back(unit, recip, ref[...])

    for descriptor in started:
        descriptor.wait_send()
    for place in range(N_PLACE):
        give_back(place).wait_send()


def per_device(images, texts, lang_order, position, logit_scale, logit_bias):
    rows, width = images.shape
    ids = jnp.broadcast_to(lang_order[None, :], (8, rows))
    vmem = pl.BlockSpec(memory_space=pltpu.VMEM)
    smem = pl.BlockSpec(memory_space=pltpu.SMEM)
    return pl.pallas_call(
        kernel,
        out_shape=(
            jax.ShapeDtypeStruct((rows, width), F32),
            jax.ShapeDtypeStruct((rows, width), F32),
            jax.ShapeDtypeStruct((1,), F32),
        ),
        in_specs=[vmem, vmem, vmem, smem, smem],
        out_specs=(vmem, vmem, smem),
        scratch_shapes=[
            pltpu.VMEM((16 * rows, width), BF16),
            pltpu.VMEM((8 * rows, width), BF16),
            pltpu.VMEM((8, 8, rows), jnp.int32),
            pltpu.VMEM((16 * rows, width), F32),
            pltpu.VMEM((8 * rows, width), F32),
            pltpu.VMEM((8 * rows, width), F32),
            pltpu.VMEM((2 * rows, 8 * rows), BF16),
            pltpu.VMEM((14, rows, width), jnp.int16),
            pltpu.VMEM((14, 8, rows), F32),
            pltpu.VMEM((14, rows, width), jnp.int16),
            pltpu.VMEM((14, 8, rows), F32),
            pltpu.VMEM((5, 8, 128), F32),
            pltpu.VMEM((4, 4, 8, 128), F32),
            pltpu.SemaphoreType.DMA((N_FLOW,)),
            pltpu.SemaphoreType.DMA((N_FLOW,)),
        ],
        compiler_params=pltpu.CompilerParams(
            collective_id=0, has_side_effects=True, vmem_limit_bytes=62 * 1024 * 1024
        ),
        name="pair_grads",
    )(images, texts, ids, logit_scale, logit_bias)


def solution(mesh):
    finer = Mesh(mesh.devices.reshape(4, 2, 4, 4), AXES)
    return jax.shard_map(
        per_device,
        mesh=finer,
        in_specs=(P(AXES, None), P(AXES, None), P(AXES), P(AXES), P(), P()),
        out_specs=(P(AXES, None), P(AXES, None), P()),
        check_vma=False,
    )
```

time: 263 us -> 110 us (0.42)
  waiting for transfers between devices: 121 us -> 0 us
  Pallas kernels: 0 us -> 102 us
  blocking collectives: 76.5 us -> 0 us
  matrix products: 33.5 us -> 0 us
  other arithmetic: 13.3 us -> 0 us
  between operations: 16.9 us -> 3.73 us
    pallas_call x0 -> x1, Pallas kernels: none -> 102 us  [per_device(): pl.pallas_call(kernel, out_shape=(jax.ShapeDtypeStruct((rows, width), F32...]
    all_gather x2 -> x0, waiting for transfers between devices: 69.8 us -> none  [the longest x1 57.3 us: per_device(): lax.all_gather(img_unit.astype(jnp.bfloat16), DEV, axis=0, tiled=True)]
    psum x1 -> x0, blocking collectives: 65.9 us -> none  [per_device(): loss = (lax.psum(loss_part, GROUP_DEV) / (total * total)).reshape(1)]
    reduce_scatter x2 -> x0, waiting for transfers between devices: 50.7 us -> none  [the longest x1 50.7 us: per_device(): lax.psum_scatter(dimg_part, DEV, scatter_dimension=0, tiled=True)]
    dot_general x3 -> x0, matrix products: 33.5 us -> none  [the longest x1 16.4 us: per_device(): lax.dot_general(img_block, txt_block, (((1,), (1,)), ((), ())), preferred...]
    all_gather x1 -> x0, blocking collectives: 10.6 us -> none  [per_device(): lax.all_gather(group_index * span + lang_order, GROUP, axis=0, tiled=True)]
    reduce_sum x4 -> x0, other arithmetic: 4.81 us -> none  [the longest x2 2.6 us: project_back(): return recip * (grad - unit * jnp.sum(unit * grad, axis=1, keepdims=True))]
    mul x2 -> x0, other arithmetic: 4.21 us -> none  [project_back(): return recip * (grad - unit * jnp.sum(unit * grad, axis=1, keepdims=True))]
  transfers between devices with their start and end apart: 4 -> 0, of which waited for: 3 -> 0; matrix products, arithmetic and copies ran while one was open for 6% -> 0% of each run, Pallas kernels for 0% -> 0%
where the time goes in v2:
time: 110 us; the launch traced here: 109 us
  Pallas kernels  102 us (93%)
  between operations  3.73 us (3%)
  local copies, waits for them, and re-layouts  3.4 us (3%)
    pallas_call x1, Pallas kernels, per_device(): pl.pallas_call(kernel, out_shape=(jax.ShapeDtypeStruct((rows, width), F32...  102 us
    unnamed x6, local copies, waits for them, and re-layouts  2.8 us

profile of v2, /device:TPU:0, one launch (start us, length us, event | category | flops | bytes accessed | tf_op | source)
XLA Modules:
  0.0 109.5 jit_solution(8176401808321346945)
XLA Ops:
  1.3 0.0 copy-start.1
  1.9 0.0 copy-done.1
  2.0 0.6 broadcast_in_dim.2.ids_in
  2.6 102.4 %pair_grads.1 = (f32[128,1152]{1,0:T(8,128)}, f32[128,1152]{1,0:T(8,128)}, f32[1]{0:T(128)}) custom-call(bf16[128,1152]{1,0:T(8,128)(2,1)} %img_in.1, bf16[128,1152]{1,0:T(8,128)(2,1)} %txt_in.1, s32[8,128]{1,0:T(8,128)} %broadcast_in_dim.2.ids_in, f32[1]{0:T(128)S(6)} %copy.11.scale_ref, f32[1]{0:T(128)S(6)} %copy.12.bias_ref), custom_call_target="tpu_custom_call" | custom-call | tf_op jit(solution)/shard_map/pair_grads/pallas_call | solution.py:340
  104.9 0.0 copy-start
  104.9 2.0 %copy.13 = f32[128,1152]{1,0:T(8,128)} copy(f32[128,1152]{1,0:T(8,128)} %get-tuple-element.6) | data formatting | bytes 1179648
  106.9 0.0 copy-done
  106.9 0.8 copy.14
Async XLA Ops:
  1.3 0.7 copy-start.1
  104.9 2.0 %copy-start = (f32[128,1152]{1,0:T(8,128)S(1)}, f32[128,1152]{1,0:T(8,128)}, u32[]{:S(2)}) copy-start(f32[128,1152]{1,0:T(8,128)} %get-tuple-element.7) | copy-start | bytes 1769476

commit v3 on v2

v3 whole, which is shorter than its diff:
```python
import jax
import jax.numpy as jnp
from jax import lax
from jax.experimental import pallas as pl
from jax.experimental.pallas import tpu as pltpu
from jax.sharding import Mesh
from jax.sharding import PartitionSpec as P

AXES = ("x", "core", "y", "z")
MESH = pl.DeviceIdType.MESH
EPSILON = 1e-06
ROWS = 128
BF16 = jnp.bfloat16
F32 = jnp.float32

PLACES = ((0, 0), (0, 1), (1, 0), (3, 0), (1, 1), (3, 1), (2, 0), (2, 1))
AT = {place: index for index, place in enumerate(PLACES)}
N_PLACE = len(PLACES)

HALVES = (0, 1)
HALF = ROWS // 2
GATHER = ("z", "plus_own", "minus_own", "plus_par", "minus_par", "plus_far", "minus_far")
REDUCE = ("far_plus", "far_minus", "near_plus", "near_minus", "relay_plus", "relay_minus", "z")
FLOWS = {}
for name in GATHER:
    FLOWS["ids", name] = len(FLOWS)
    for part in HALVES:
        for kind in ("img", "txt"):
            FLOWS[kind, name, part] = len(FLOWS)
for kind in ("dimg", "dimg_s", "dtxt", "dtxt_s"):
    for name in REDUCE:
        for part in HALVES:
            FLOWS[kind, name, part] = len(FLOWS)
for place in range(N_PLACE):
    FLOWS["share", place] = len(FLOWS)
for place in range(N_PLACE):
    FLOWS["swap", place] = len(FLOWS)
FLOWS["loss_core"] = len(FLOWS)
for axis in ("x", "y", "z"):
    for step in (1, 2, 3):
        FLOWS["loss", axis, step] = len(FLOWS)
N_FLOW = len(FLOWS)


def normalize(values):
    wide = values.astype(F32)
    recip = lax.rsqrt(jnp.sum(wide * wide, axis=1, keepdims=True) + EPSILON)
    return (wide * recip, recip)


def project_back(unit, recip, grad):
    return recip * (grad - unit * jnp.sum(unit * grad, axis=1, keepdims=True))


def tile_at(index):
    table = (
        (8, 4, lambda k: 7 - k // 4, lambda k: 3 - k % 4),
        (14, 1, lambda k: 5 - k, lambda k: 3),
        (20, 3, lambda k: 5 - k // 3, lambda k: 2 - k % 3),
        (24, 1, lambda k: 3 - k, lambda k: 2),
        (32, 2, lambda k: 3 - k // 2, lambda k: 1 - k % 2),
    )
    first = 0
    pair, group = jnp.int32(0), jnp.int32(0)
    for last, _, pair_of, group_of in table:
        inside = jnp.logical_and(index >= first, index < last)
        pair = jnp.where(inside, pair_of(index - first), pair)
        group = jnp.where(inside, group_of(index - first), group)
        first = last
    return pair, group


def kernel(
    img_in, txt_in, ids_in, scale_ref, bias_ref,
    img_out, txt_out, loss_out,
    img_raw, txt_raw, ids_raw,
    img, txt, ids, dimg, swap, dtxt, coeff, sent, sent_s, got, got_s, loss_tile, loss_got,
    load_sem, send_sem, recv_sem,
):
    x, core = lax.axis_index("x"), lax.axis_index("core")
    y, z = lax.axis_index("y"), lax.axis_index("z")
    other = {"core": 1 - core}
    z_img = z + 1 - 2 * lax.rem(z, 2)
    z_txt = 3 - z
    plus = {"img": {"x": lax.rem(x + 1, 4)}, "txt": {"y": lax.rem(y + 1, 4)}}
    minus = {"img": {"x": lax.rem(x + 3, 4)}, "txt": {"y": lax.rem(y + 3, 4)}}
    across = {"img": {"z": z_img}, "txt": {"z": z_txt}}

    loads = [
        pltpu.make_async_copy(src, dst, load_sem.at[number])
        for number, (src, dst) in enumerate(
            ((img_in, img_raw), (txt_in, txt_raw), (ids_in, ids_raw))
        )
    ]
    for load in loads:
        load.start()

    started = []

    def copy(flow, src, dst, device):
        return pltpu.make_async_remote_copy(
            src_ref=src, dst_ref=dst, send_sem=send_sem.at[flow], recv_sem=recv_sem.at[flow],
            device_id=device, device_id_type=MESH,
        )

    def launch(make):
        make().start()
        started.append(make)

    barrier = pltpu.get_barrier_semaphore()
    peers = [other]
    for axis, here in (("x", x), ("y", y), ("z", z)):
        for step in (1, 2, 3):
            peers.append({axis: lax.rem(here + step, 4)})
    for peer in peers:
        pl.semaphore_signal(barrier, inc=1, device_id=peer, device_id_type=MESH)

    def img_rows(place, which):
        return pl.ds((2 * place + which) * ROWS, ROWS)

    def rows(place):
        return pl.ds(place * ROWS, ROWS)

    for load in loads:
        load.wait()
    img[img_rows(0, 0), :] = normalize(img_raw[...])[0].astype(BF16)
    txt[rows(0), :] = normalize(txt_raw[...])[0].astype(BF16)
    ids[0] = jnp.broadcast_to(ids_raw[...], (8, ROWS))
    scale = scale_ref[0]
    bias = bias_ref[0]
    pl.semaphore_wait(barrier, len(peers))

    def gather(kind, name, part):
        ring = "img" if kind == "img" else "txt"
        src, dst, device = {
            "z": ((0, 0), (0, 1), across[ring]),
            "plus_own": ((0, 0), (3, 0), plus[ring]),
            "minus_own": ((0, 0), (1, 0), minus[ring]),
            "plus_par": ((0, 1), (3, 1), plus[ring]),
            "minus_par": ((0, 1), (1, 1), minus[ring]),
            "plus_far": ((3, 0), (2, 0), plus[ring]),
            "minus_far": ((1, 1), (2, 1), minus[ring]),
        }[name]
        src, dst = AT[src], AT[dst]
        if kind == "ids":
            return copy(FLOWS[kind, name], ids.at[src], ids.at[dst], device)
        ref, every = (img, 2) if kind == "img" else (txt, 1)
        return copy(
            FLOWS[kind, name, part],
            ref.at[pl.ds(src * every * ROWS + part * HALF, HALF), :],
            ref.at[pl.ds(dst * every * ROWS + part * HALF, HALF), :],
            device,
        )

    def share(place):
        return copy(
            FLOWS["share", place], img.at[img_rows(place, 0), :], img.at[img_rows(place, 1), :], other
        )

    def go(kind, name, part):
        launch(lambda: gather(kind, name, part))
        if kind == "txt" and part == 1:
            launch(lambda: gather("ids", name, 0))

    def give(place):
        launch(lambda: share(AT[place]))

    def come(kind, name, part):
        gather(kind, name, part).wait_recv()
        if kind == "txt" and part == 1:
            gather("ids", name, 0).wait_recv()

    for part in HALVES:
        for name in ("z", "plus_own", "minus_own"):
            go("img", name, part)
            go("txt", name, part)
    give((0, 0))
    dimg[...] = jnp.zeros_like(dimg)
    dtxt[...] = jnp.zeros_like(dtxt)
    loss_tile[0] = jnp.zeros_like(loss_tile[0])
    for part in HALVES:
        for kind in ("img", "txt"):
            come(kind, "z", part)
            go(kind, "plus_par", part)
            go(kind, "minus_par", part)
        for kind in ("img", "txt"):
            come(kind, "plus_own", part)
            go(kind, "plus_far", part)
    give((0, 1))
    give((3, 0))
    for part in HALVES:
        come("img", "minus_own", part)
        come("txt", "minus_own", part)
    give((1, 0))
    for part in HALVES:
        for kind in ("img", "txt"):
            come(kind, "minus_par", part)
            go(kind, "minus_far", part)
    give((1, 1))
    for part in HALVES:
        come("img", "plus_par", part)
        come("txt", "plus_par", part)
    give((3, 1))
    for name, place in (("plus_far", (2, 0)), ("minus_far", (2, 1))):
        for part in HALVES:
            come("img", name, part)
        give(place)
    for name in ("plus_far", "minus_far"):
        for part in HALVES:
            come("txt", name, part)
    for place in range(N_PLACE):
        share(place).wait_recv()

    eye = lax.broadcasted_iota(jnp.int32, (HALF, ROWS), 0) == lax.broadcasted_iota(
        jnp.int32, (HALF, ROWS), 1
    )

    def give_back(place):
        return copy(
            FLOWS["swap", place], dimg.at[img_rows(place, 1), :], swap.at[rows(place), :], other
        )

    def slot(kind, name, part):
        number = REDUCE.index(name) + (0 if kind == "dimg" else len(REDUCE))
        return number * 2 + part

    def sum_ref(kind, place, part):
        if kind == "dimg":
            return dimg.at[pl.ds(AT[place] * 2 * ROWS + part * HALF, HALF), :]
        return dtxt.at[pl.ds(AT[place] * ROWS + part * HALF, HALF), :]

    def route(kind, name):
        ring = "img" if kind == "dimg" else "txt"
        if name == "z":
            return across[ring]
        return plus[ring] if name.endswith("plus") else minus[ring]

    def values(kind, name, part):
        s = slot(kind, name, part)
        return copy(FLOWS[kind, name, part], sent.at[s], got.at[s], route(kind, name))

    def units(kind, name, part):
        s = slot(kind, name, part)
        return copy(FLOWS[kind + "_s", name, part], sent_s.at[s], got_s.at[s], route(kind, name))

    def send(kind, name, place, part):
        ref = sum_ref(kind, place, part)
        s = slot(kind, name, part)
        top = jnp.maximum(jnp.max(jnp.abs(ref[...]), axis=1, keepdims=True), 1e-30)
        across_lanes = jnp.sum(jnp.where(eye, top * (1.0 / 32767.0), 0.0), axis=0, keepdims=True)
        sent_s[s] = jnp.broadcast_to(across_lanes, (8, ROWS))
        sent[s] = jnp.round(ref[...] * (32767.0 / top)).astype(jnp.int32).astype(jnp.int16)
        launch(lambda: values(kind, name, part))
        launch(lambda: units(kind, name, part))

    def take(kind, name, part):
        s = slot(kind, name, part)
        values(kind, name, part).wait_recv()
        units(kind, name, part).wait_recv()
        unit = jnp.sum(jnp.where(eye, got_s[s, 0:1, :], 0.0), axis=1, keepdims=True)
        return got[s].astype(jnp.int32).astype(F32) * unit

    def add(kind, name, place, part):
        sum_ref(kind, place, part)[...] += take(kind, name, part)

    def merge(place):
        give_back(AT[place]).wait_recv()
        dimg[img_rows(AT[place], 0), :] += swap[rows(AT[place]), :]

    def relay(kind, way, place):
        for part in HALVES:
            add(kind, "far_" + way, place, part)
            send(kind, "relay_" + way, place, part)

    def send_all(kind, name, place):
        for part in HALVES:
            send(kind, name, place, part)

    row_iota = lax.broadcasted_iota(jnp.int32, (2 * ROWS, 1), 0)

    def spans(index):
        pair, group = tile_at(index)
        return (
            pair,
            pl.ds(pl.multiple_of(pair * (2 * ROWS), 2 * ROWS), 2 * ROWS),
            group,
            pl.ds(pl.multiple_of(group * (2 * ROWS), 2 * ROWS), 2 * ROWS),
        )

    def make_coeff(index):
        pair, here, group, there = spans(index)
        logits = scale * lax.dot_general(
            img[here, :], txt[there, :], (((1,), (1,)), ((), ())), preferred_element_type=F32
        ) + bias
        owner = jnp.where(pair == 0, y * 4 + z, y * 4 + z_img) * ROWS
        valid = jnp.logical_and(pair < 2, row_iota < ROWS)
        row_ids = jnp.where(valid, owner + row_iota, -1)
        column_ids = jnp.concatenate(
            [ids[2 * group, 0:1, :], ids[2 * group + 1, 0:1, :]], axis=1
        )
        same = row_ids == column_ids
        logits = jnp.where(same, -logits, logits)
        small = jnp.exp(-jnp.abs(logits))
        one_plus = 1.0 + small
        recip = 1.0 / one_plus
        sigmoid = jnp.where(logits >= 0, recip, small * recip)
        log1p = jnp.where(
            small < 0.01,
            small * (1.0 - small * (0.5 - small * (1.0 / 3.0))),
            jnp.log(one_plus),
        )
        softplus = jnp.maximum(logits, 0.0) + log1p
        folded = jnp.sum(softplus.reshape(32, 8, 256), axis=0)
        loss_tile[0] += folded[:, :128] + folded[:, 128:]
        coeff[lax.rem(index, 2)] = jnp.where(same, -sigmoid, sigmoid).astype(BF16)

    def use_coeff(index):
        _, here, _, there = spans(index)
        half = coeff[lax.rem(index, 2)]
        dimg[here, :] += jnp.dot(half, txt[there, :], preferred_element_type=F32)
        dtxt[there, :] += lax.dot_general(
            half, img[here, :], (((0,), (0,)), ((), ())), preferred_element_type=F32
        )

    def pass_back(place):
        launch(lambda: give_back(place))

    def far_dimg():
        merge((2, 1))
        send_all("dimg", "far_minus", (2, 1))
        merge((2, 0))
        send_all("dimg", "far_plus", (2, 0))

    def far_dtxt():
        send_all("dtxt", "far_minus", (2, 1))
        send_all("dtxt", "far_plus", (2, 0))

    def near_dimg():
        merge((1, 1))
        merge((3, 1))
        send_all("dimg", "near_plus", (1, 1))

    events = {
        3: lambda: pass_back(7),
        7: lambda: pass_back(6),
        10: far_dimg,
        13: far_dtxt,
        16: lambda: pass_back(5),
        19: lambda: pass_back(4),
        21: near_dimg,
        23: lambda: send_all("dtxt", "near_plus", (1, 1)),
        25: lambda: pass_back(3),
        27: lambda: pass_back(2),
        28: lambda: relay("dimg", "minus", (3, 1)),
        29: lambda: pass_back(1),
    }

    make_coeff(jnp.int32(0))

    def step(index, carry):
        make_coeff(index + 1)
        use_coeff(index)
        for moment, event in events.items():
            pl.when(index == moment)(event)
        return carry

    lax.fori_loop(0, 31, step, 0)
    use_coeff(jnp.int32(31))
    pass_back(0)

    def loss_send(axis, here, number):
        loss_got[number, here] = loss_tile[number]
        for stride in (1, 2, 3):
            launch(
                lambda stride=stride: copy(
                    FLOWS["loss", axis, stride], loss_tile.at[number], loss_got.at[number, here],
                    {axis: lax.rem(here + stride, 4)},
                )
            )

    def loss_take(axis, here, number):
        for stride in (1, 2, 3):
            source = lax.rem(here + 4 - stride, 4)
            copy(
                FLOWS["loss", axis, stride], loss_tile.at[number], loss_got.at[number, source],
                {axis: lax.rem(here + stride, 4)},
            ).wait_recv()
        loss_tile[number + 1] = (loss_got[number, 0] + loss_got[number, 1]) + (
            loss_got[number, 2] + loss_got[number, 3]
        )

    def loss_swap():
        return copy(FLOWS["loss_core"], loss_tile.at[0], loss_got.at[0, 0], other)

    launch(loss_swap)
    merge((3, 0))
    send_all("dimg", "near_minus", (3, 0))
    relay("dtxt", "minus", (3, 1))
    loss_swap().wait_recv()
    loss_tile[1] = loss_tile[0] + loss_got[0, 0]
    loss_send("x", x, 1)
    merge((1, 0))
    relay("dimg", "plus", (1, 0))
    relay("dtxt", "plus", (1, 0))
    send_all("dtxt", "near_minus", (3, 0))
    merge((0, 1))
    merge((0, 0))
    loss_take("x", x, 1)
    loss_send("y", y, 2)
    for kind in ("dimg", "dtxt"):
        for part in HALVES:
            add(kind, "near_plus", (0, 1), part)
    for kind in ("dimg", "dtxt"):
        for part in HALVES:
            add(kind, "relay_minus", (0, 1), part)
            send(kind, "z", (0, 1), part)
    loss_take("y", y, 2)
    loss_send("z", z, 3)
    for name in ("near_minus", "relay_plus"):
        for kind in ("dimg", "dtxt"):
            for part in HALVES:
                add(kind, name, (0, 0), part)
    loss_take("z", z, 3)
    count = F32(ROWS * 128)
    loss_out[0] = jnp.sum(loss_tile[4]) / (count * count)
    for kind, source, out in (("dimg", img_raw, img_out), ("dtxt", txt_raw, txt_out)):
        for part in HALVES:
            ref = sum_ref(kind, (0, 0), part)
            piece = pl.ds(part * HALF, HALF)
            ref[...] = scale * (ref[...] + take(kind, "z", part))
            unit, recip = normalize(source[piece, :])
            out[piece, :] = project_back(unit, recip, ref[...])

    for make in started:
        make().wait_send()


def per_device(images, texts, lang_order, position, logit_scale, logit_bias):
    rows, width = images.shape
    ids = lang_order.reshape(1, rows)
    whole = pl.BlockSpec(memory_space=pl.ANY)
    vmem = pl.BlockSpec(memory_space=pltpu.VMEM)
    smem = pl.BlockSpec(memory_space=pltpu.SMEM)
    return pl.pallas_call(
        kernel,
        out_shape=(
            jax.ShapeDtypeStruct((rows, width), F32),
            jax.ShapeDtypeStruct((rows, width), F32),
            jax.ShapeDtypeStruct((1,), F32),
        ),
        in_specs=[whole, whole, whole, smem, smem],
        out_specs=(vmem, vmem, smem),
        scratch_shapes=[
            pltpu.VMEM((rows, width), BF16),
            pltpu.VMEM((rows, width), BF16),
            pltpu.VMEM((1, rows), jnp.int32),
            pltpu.VMEM((16 * rows, width), BF16),
            pltpu.VMEM((8 * rows, width), BF16),
            pltpu.VMEM((8, 8, rows), jnp.int32),
            pltpu.VMEM((16 * rows, width), F32),
            pltpu.VMEM((8 * rows, width), F32),
            pltpu.VMEM((8 * rows, width), F32),
            pltpu.VMEM((2, 2 * rows, 2 * rows), BF16),
            pltpu.VMEM((28, HALF, width), jnp.int16),
            pltpu.VMEM((28, 8, rows), F32),
            pltpu.VMEM((28, HALF, width), jnp.int16),
            pltpu.VMEM((28, 8, rows), F32),
            pltpu.VMEM((5, 8, 128), F32),
            pltpu.VMEM((4, 4, 8, 128), F32),
            pltpu.SemaphoreType.DMA((3,)),
            pltpu.SemaphoreType.DMA((N_FLOW,)),
            pltpu.SemaphoreType.DMA((N_FLOW,)),
        ],
        compiler_params=pltpu.CompilerParams(
            collective_id=0, has_side_effects=True, vmem_limit_bytes=62 * 1024 * 1024
        ),
        name="pair_grads",
    )(images, texts, ids, logit_scale, logit_bias)


def solution(mesh):
    finer = Mesh(mesh.devices.reshape(4, 2, 4, 4), AXES)
    return jax.shard_map(
        per_device,
        mesh=finer,
        in_specs=(P(AXES, None), P(AXES, None), P(AXES), P(AXES), P(), P()),
        out_specs=(P(AXES, None), P(AXES, None), P()),
        check_vma=False,
    )
```

time: 110 us -> 108 us (0.982)
    pallas_call x1, Pallas kernels: 102 us -> 101 us  [per_device(): pl.pallas_call(kernel, out_shape=(jax.ShapeDtypeStruct((rows, width), F32...]
    unnamed x6 -> x4, local copies, waits for them, and re-layouts: 2.8 us -> 2.8 us
where the time goes in v3:
time: 108 us; the launch traced here: 107 us
  Pallas kernels  101 us (94%)
  between operations  3.67 us (3%)
  local copies, waits for them, and re-layouts  2.8 us (3%)
    pallas_call x1, Pallas kernels, per_device(): pl.pallas_call(kernel, out_shape=(jax.ShapeDtypeStruct((rows, width), F32...  101 us
    unnamed x4, local copies, waits for them, and re-layouts  2.8 us

profile of v3, /device:TPU:0, one launch (start us, length us, event | category | flops | bytes accessed | tf_op | source)
XLA Modules:
  0.0 107.3 jit_solution(16728014815753347626)
XLA Ops:
  1.9 100.9 %pair_grads.1 = (f32[128,1152]{1,0:T(8,128)}, f32[128,1152]{1,0:T(8,128)}, f32[1]{0:T(128)}) custom-call(bf16[128,1152]{1,0:T(8,128)(2,1)} %img_in.1, bf16[128,1152]{1,0:T(8,128)(2,1)} %txt_in.1, s32[1,128]{1,0:T(1,128)} %bitcast.1, f32[1]{0:T(128)S(6)} %copy.11.scale_ref, f32[1]{0:T(128)S(6)} %copy.12.bias_ref), custom_call_target="tpu_custom_call" | custom-call | tf_op jit(solution)/shard_map/pair_grads/pallas_call | solution.py:444
  102.8 0.0 copy-start
  102.8 2.0 %copy.13 = f32[128,1152]{1,0:T(8,128)} copy(f32[128,1152]{1,0:T(8,128)} %get-tuple-element.6) | data formatting | bytes 1179648
  104.8 0.0 copy-done
  104.8 0.8 copy.14
Async XLA Ops:
  102.8 2.0 %copy-start = (f32[128,1152]{1,0:T(8,128)S(1)}, f32[128,1152]{1,0:T(8,128)}, u32[]{:S(2)}) copy-start(f32[128,1152]{1,0:T(8,128)} %get-tuple-element.7) | copy-start | bytes 1769476

commit v4 on v3

--- a/solution.py
+++ b/solution.py
@@ -58,7 +58,6 @@
         (14, 1, lambda k: 5 - k, lambda k: 3),
         (20, 3, lambda k: 5 - k // 3, lambda k: 2 - k % 3),
         (24, 1, lambda k: 3 - k, lambda k: 2),
-        (32, 2, lambda k: 3 - k // 2, lambda k: 1 - k % 2),
     )
     first = 0
     pair, group = jnp.int32(0), jnp.int32(0)
@@ -73,8 +72,8 @@
 def kernel(
     img_in, txt_in, ids_in, scale_ref, bias_ref,
     img_out, txt_out, loss_out,
-    img_raw, txt_raw, ids_raw,
-    img, txt, ids, dimg, swap, dtxt, coeff, sent, sent_s, got, got_s, loss_tile, loss_got,
+    img_raw, txt_raw, ids_raw, scale_raw, bias_raw,
+    img, txt, ids, dimg, swap, dtxt, even, odd, kept, sent, sent_s, got, got_s, loss_tile, loss_got,
     load_sem, send_sem, recv_sem,
 ):
     x, core = lax.axis_index("x"), lax.axis_index("core")
@@ -89,7 +88,10 @@
     loads = [
         pltpu.make_async_copy(src, dst, load_sem.at[number])
         for number, (src, dst) in enumerate(
-            ((img_in, img_raw), (txt_in, txt_raw), (ids_in, ids_raw))
+            (
+                (img_in, img_raw), (txt_in, txt_raw), (ids_in, ids_raw),
+                (scale_ref, scale_raw), (bias_ref, bias_raw),
+            )
         )
     ]
     for load in loads:
@@ -126,8 +128,8 @@
     img[img_rows(0, 0), :] = normalize(img_raw[...])[0].astype(BF16)
     txt[rows(0), :] = normalize(txt_raw[...])[0].astype(BF16)
     ids[0] = jnp.broadcast_to(ids_raw[...], (8, ROWS))
-    scale = scale_ref[0]
-    bias = bias_ref[0]
+    scale = scale_raw[0]
+    bias = bias_raw[0]
     pl.semaphore_wait(barrier, len(peers))
 
     def gather(kind, name, part):
@@ -169,6 +171,40 @@
         gather(kind, name, part).wait_recv()
         if kind == "txt" and part == 1:
             gather("ids", name, 0).wait_recv()
+
+    row_iota = lax.broadcasted_iota(jnp.int32, (2 * ROWS, 1), 0)
+
+    def span(number):
+        return pl.ds(pl.multiple_of(number * (2 * ROWS), 2 * ROWS), 2 * ROWS)
+
+    def make_coeff(pair, group):
+        logits = scale * lax.dot_general(
+            img[span(pair), :], txt[span(group), :], (((1,), (1,)), ((), ())),
+            preferred_element_type=F32,
+        ) + bias
+        owner = jnp.where(pair == 0, y * 4 + z, y * 4 + z_img) * ROWS
+        valid = jnp.logical_and(pair < 2, row_iota < ROWS)
+        row_ids = jnp.where(valid, owner + row_iota, -1)
+        column_ids = jnp.concatenate(
+            [ids[2 * group, 0:1, :], ids[2 * group + 1, 0:1, :]], axis=1
+        )
+        same = row_ids == column_ids
+        logits = jnp.where(same, -logits, logits)
+        power = jnp.exp(logits)
+        one_plus = 1.0 + power
+        recip = 1.0 / one_plus
+        sigmoid = power * recip
+        softplus = jnp.log(one_plus) + (power - (one_plus - 1.0)) * recip
+        folded = jnp.sum(softplus.reshape(32, 8, 256), axis=0)
+        loss_tile[0] += folded[:, :128] + folded[:, 128:]
+        return jnp.where(same, -sigmoid, sigmoid).astype(BF16)
+
+    def use_coeff(half, pair, group):
+        here, there = span(pair), span(group)
+        dimg[here, :] += jnp.dot(half, txt[there, :], preferred_element_type=F32)
+        dtxt[there, :] += lax.dot_general(
+            half, img[here, :], (((0,), (0,)), ((), ())), preferred_element_type=F32
+        )
 
     for part in HALVES:
         for name in ("z", "plus_own", "minus_own"):
@@ -192,6 +228,15 @@
         come("img", "minus_own", part)
         come("txt", "minus_own", part)
     give((1, 0))
+
+    for place in range(4):
+        share(place).wait_recv()
+
+    def early(index, carry):
+        kept[index] = make_coeff(3 - index // 2, 1 - lax.rem(index, 2))
+        return carry
+
+    lax.fori_loop(0, 8, early, 0)
     for part in HALVES:
         for kind in ("img", "txt"):
             come(kind, "minus_par", part)
@@ -208,7 +253,7 @@
     for name in ("plus_far", "minus_far"):
         for part in HALVES:
             come("txt", name, part)
-    for place in range(N_PLACE):
+    for place in range(4, N_PLACE):
         share(place).wait_recv()
 
     eye = lax.broadcasted_iota(jnp.int32, (HALF, ROWS), 0) == lax.broadcasted_iota(
@@ -217,7 +262,7 @@
 
     def give_back(place):
         return copy(
-            FLOWS["swap", place], dimg.at[img_rows(place, 1), :], swap.at[rows(place), :], other
+            FLOWS["swap", 0] + place, dimg.at[img_rows(place, 1), :], swap.at[rows(place), :], other
         )
 
     def slot(kind, name, part):
@@ -276,52 +321,6 @@
         for part in HALVES:
             send(kind, name, place, part)
 
-    row_iota = lax.broadcasted_iota(jnp.int32, (2 * ROWS, 1), 0)
-
-    def spans(index):
-        pair, group = tile_at(index)
-        return (
-            pair,
-            pl.ds(pl.multiple_of(pair * (2 * ROWS), 2 * ROWS), 2 * ROWS),
-            group,
-            pl.ds(pl.multiple_of(group * (2 * ROWS), 2 * ROWS), 2 * ROWS),
-        )
-
-    def make_coeff(index):
-        pair, here, group, there = spans(index)
-        logits = scale * lax.dot_general(
-            img[here, :], txt[there, :], (((1,), (1,)), ((), ())), preferred_element_type=F32
-        ) + bias
-        owner = jnp.where(pair == 0, y * 4 + z, y * 4 + z_img) * ROWS
-        valid = jnp.logical_and(pair < 2, row_iota < ROWS)
-        row_ids = jnp.where(valid, owner + row_iota, -1)
-        column_ids = jnp.concatenate(
-            [ids[2 * group, 0:1, :], ids[2 * group + 1, 0:1, :]], axis=1
-        )
-        same = row_ids == column_ids
-        logits = jnp.where(same, -logits, logits)
-        small = jnp.exp(-jnp.abs(logits))
-        one_plus = 1.0 + small
-        recip = 1.0 / one_plus
-        sigmoid = jnp.where(logits >= 0, recip, small * recip)
-        log1p = jnp.where(
-            small < 0.01,
-            small * (1.0 - small * (0.5 - small * (1.0 / 3.0))),
-            jnp.log(one_plus),
-        )
-        softplus = jnp.maximum(logits, 0.0) + log1p
-        folded = jnp.sum(softplus.reshape(32, 8, 256), axis=0)
-        loss_tile[0] += folded[:, :128] + folded[:, 128:]
-        coeff[lax.rem(index, 2)] = jnp.where(same, -sigmoid, sigmoid).astype(BF16)
-
-    def use_coeff(index):
-        _, here, _, there = spans(index)
-        half = coeff[lax.rem(index, 2)]
-        dimg[here, :] += jnp.dot(half, txt[there, :], preferred_element_type=F32)
-        dtxt[there, :] += lax.dot_general(
-            half, img[here, :], (((0,), (0,)), ((), ())), preferred_element_type=F32
-        )
-
     def pass_back(place):
         launch(lambda: give_back(place))
 
@@ -334,39 +333,6 @@
     def far_dtxt():
         send_all("dtxt", "far_minus", (2, 1))
         send_all("dtxt", "far_plus", (2, 0))
-
-    def near_dimg():
-        merge((1, 1))
-        merge((3, 1))
-        send_all("dimg", "near_plus", (1, 1))
-
-    events = {
-        3: lambda: pass_back(7),
-        7: lambda: pass_back(6),
-        10: far_dimg,
-        13: far_dtxt,
-        16: lambda: pass_back(5),
-        19: lambda: pass_back(4),
-        21: near_dimg,
-        23: lambda: send_all("dtxt", "near_plus", (1, 1)),
-        25: lambda: pass_back(3),
-        27: lambda: pass_back(2),
-        28: lambda: relay("dimg", "minus", (3, 1)),
-        29: lambda: pass_back(1),
-    }
-
-    make_coeff(jnp.int32(0))
-
-    def step(index, carry):
-        make_coeff(index + 1)
-        use_coeff(index)
-        for moment, event in events.items():
-            pl.when(index == moment)(event)
-        return carry
-
-    lax.fori_loop(0, 31, step, 0)
-    use_coeff(jnp.int32(31))
-    pass_back(0)
 
     def loss_send(axis, here, number):
         loss_got[number, here] = loss_tile[number]
@@ -392,35 +358,83 @@
     def loss_swap():
         return copy(FLOWS["loss_core"], loss_tile.at[0], loss_got.at[0, 0], other)
 
+    events = {
+        1: lambda: pass_back(7),
+        3: lambda: pass_back(6),
+        5: far_dimg,
+        6: far_dtxt,
+        8: lambda: pass_back(5),
+        9: lambda: pass_back(4),
+    }
+
+    def make(index, buffer):
+        buffer[...] = make_coeff(*tile_at(index))
+
+    def use(index, buffer):
+        use_coeff(buffer[...], *tile_at(index))
+
+    make(jnp.int32(0), even)
+
+    def step(index, carry):
+        make(2 * index + 1, odd)
+        use(2 * index, even)
+        make(2 * index + 2, even)
+        use(2 * index + 1, odd)
+        for moment, event in events.items():
+            pl.when(index == moment)(event)
+        return carry
+
+    lax.fori_loop(0, 11, step, 0)
+    make(jnp.int32(23), odd)
     launch(loss_swap)
+    use(jnp.int32(22), even)
+    use(jnp.int32(23), odd)
+
+    merge((3, 1))
+    relay("dimg", "minus", (3, 1))
+    merge((1, 1))
+    send_all("dimg", "near_plus", (1, 1))
+    loss_swap().wait_recv()
+    loss_tile[1] = loss_tile[0] + loss_got[0, 0]
+    loss_send("y", y, 1)
+    relay("dtxt", "minus", (3, 1))
+    send_all("dtxt", "near_plus", (1, 1))
+
+    def late(index, carry):
+        use_coeff(kept[2 * index], 3 - index, 1)
+        use_coeff(kept[2 * index + 1], 3 - index, 0)
+        give_back(3 - index).start()
+        return carry
+
+    lax.fori_loop(0, 2, late, 0)
+    loss_take("y", y, 1)
+    loss_send("z", z, 2)
+    lax.fori_loop(2, 4, late, 0)
+    for place in range(4):
+        started.append(lambda place=place: give_back(place))
+
+    relay("dtxt", "plus", (1, 0))
+    send_all("dtxt", "near_minus", (3, 0))
     merge((3, 0))
     send_all("dimg", "near_minus", (3, 0))
-    relay("dtxt", "minus", (3, 1))
-    loss_swap().wait_recv()
-    loss_tile[1] = loss_tile[0] + loss_got[0, 0]
-    loss_send("x", x, 1)
     merge((1, 0))
     relay("dimg", "plus", (1, 0))
-    relay("dtxt", "plus", (1, 0))
-    send_all("dtxt", "near_minus", (3, 0))
     merge((0, 1))
-    merge((0, 0))
-    loss_take("x", x, 1)
-    loss_send("y", y, 2)
     for kind in ("dimg", "dtxt"):
         for part in HALVES:
             add(kind, "near_plus", (0, 1), part)
+    loss_take("z", z, 2)
+    loss_send("x", x, 3)
     for kind in ("dimg", "dtxt"):
         for part in HALVES:
             add(kind, "relay_minus", (0, 1), part)
             send(kind, "z", (0, 1), part)
-    loss_take("y", y, 2)
-    loss_send("z", z, 3)
+    merge((0, 0))
     for name in ("near_minus", "relay_plus"):
-        for kind in ("dimg", "dtxt"):
+        for kind in ("dtxt", "dimg"):
             for part in HALVES:
                 add(kind, name, (0, 0), part)
-    loss_take("z", z, 3)
+    loss_take("x", x, 3)
     count = F32(ROWS * 128)
     loss_out[0] = jnp.sum(loss_tile[4]) / (count * count)
     for kind, source, out in (("dimg", img_raw, img_out), ("dtxt", txt_raw, txt_out)):
@@ -448,26 +462,30 @@
             jax.ShapeDtypeStruct((rows, width), F32),
             jax.ShapeDtypeStruct((1,), F32),
         ),
-        in_specs=[whole, whole, whole, smem, smem],
+        in_specs=[whole] * 5,
         out_specs=(vmem, vmem, smem),
         scratch_shapes=[
             pltpu.VMEM((rows, width), BF16),
             pltpu.VMEM((rows, width), BF16),
             pltpu.VMEM((1, rows), jnp.int32),
+            pltpu.SMEM((1,), F32),
+            pltpu.SMEM((1,), F32),
             pltpu.VMEM((16 * rows, width), BF16),
             pltpu.VMEM((8 * rows, width), BF16),
             pltpu.VMEM((8, 8, rows), jnp.int32),
             pltpu.VMEM((16 * rows, width), F32),
             pltpu.VMEM((8 * rows, width), F32),
             pltpu.VMEM((8 * rows, width), F32),
-            pltpu.VMEM((2, 2 * rows, 2 * rows), BF16),
+            pltpu.VMEM((2 * rows, 2 * rows), BF16),
+            pltpu.VMEM((2 * rows, 2 * rows), BF16),
+            pltpu.VMEM((8, 2 * rows, 2 * rows), BF16),
             pltpu.VMEM((28, HALF, width), jnp.int16),
             pltpu.VMEM((28, 8, rows), F32),
             pltpu.VMEM((28, HALF, width), jnp.int16),
             pltpu.VMEM((28, 8, rows), F32),
             pltpu.VMEM((5, 8, 128), F32),
             pltpu.VMEM((4, 4, 8, 128), F32),
-            pltpu.SemaphoreType.DMA((3,)),
+            pltpu.SemaphoreType.DMA((5,)),
             pltpu.SemaphoreType.DMA((N_FLOW,)),
             pltpu.SemaphoreType.DMA((N_FLOW,)),
         ],

time: 108 us -> 78.8 us (0.73)
  Pallas kernels: 101 us -> 72.2 us
    pallas_call x1, Pallas kernels: 101 us -> 72.2 us  [per_device(): pl.pallas_call(kernel, out_shape=(jax.ShapeDtypeStruct((rows, width), F32...]
where the time goes in v4:
time: 78.8 us; the launch traced here: 78.6 us
  Pallas kernels  72.2 us (92%)
  between operations  3.67 us (5%)
  local copies, waits for them, and re-layouts  2.8 us (4%)
    pallas_call x1, Pallas kernels, per_device(): pl.pallas_call(kernel, out_shape=(jax.ShapeDtypeStruct((rows, width), F32...  72.2 us
    unnamed x4, local copies, waits for them, and re-layouts  2.8 us

profile of v4, /device:TPU:0, one launch (start us, length us, event | category | flops | bytes accessed | tf_op | source)
XLA Modules:
  0.0 78.6 jit_solution(6606690203505510079)
XLA Ops:
  1.9 72.2 %pair_grads.1 = (f32[128,1152]{1,0:T(8,128)}, f32[128,1152]{1,0:T(8,128)}, f32[1]{0:T(128)}) custom-call(bf16[128,1152]{1,0:T(8,128)(2,1)} %img_in.1, bf16[128,1152]{1,0:T(8,128)(2,1)} %txt_in.1, s32[1,128]{1,0:T(1,128)} %bitcast.1, f32[1]{0:T(128)S(6)} %copy.11.scale_ref, f32[1]{0:T(128)S(6)} %copy.12.bias_ref), custom_call_target="tpu_custom_call" | custom-call | tf_op jit(solution)/shard_map/pair_grads/pallas_call | solution.py:458
  74.1 0.0 copy-start
  74.1 2.0 %copy.13 = f32[128,1152]{1,0:T(8,128)} copy(f32[128,1152]{1,0:T(8,128)} %get-tuple-element.6) | data formatting | bytes 1179648
  76.1 0.0 copy-done
  76.1 0.8 %copy.14 = f32[128,1152]{1,0:T(8,128)} copy(f32[128,1152]{1,0:T(8,128)S(1)} %copy-done) | data formatting | bytes 1179648
Async XLA Ops:
  74.1 2.0 %copy-start = (f32[128,1152]{1,0:T(8,128)S(1)}, f32[128,1152]{1,0:T(8,128)}, u32[]{:S(2)}) copy-start(f32[128,1152]{1,0:T(8,128)} %get-tuple-element.7) | copy-start | bytes 1769476

commit v5 on v4

--- a/solution.py
+++ b/solution.py
@@ -19,7 +19,7 @@
 
 HALVES = (0, 1)
 HALF = ROWS // 2
-GATHER = ("z", "plus_own", "minus_own", "plus_par", "minus_par", "plus_far", "minus_far")
+GATHER = ("z", "plus_own", "minus_own", "plus_par", "minus_par", "plus_far", "minus_far", "z_far")
 REDUCE = ("far_plus", "far_minus", "near_plus", "near_minus", "relay_plus", "relay_minus", "z")
 FLOWS = {}
 for name in GATHER:
@@ -54,14 +54,15 @@
 
 def tile_at(index):
     table = (
-        (8, 4, lambda k: 7 - k // 4, lambda k: 3 - k % 4),
-        (14, 1, lambda k: 5 - k, lambda k: 3),
-        (20, 3, lambda k: 5 - k // 3, lambda k: 2 - k % 3),
-        (24, 1, lambda k: 3 - k, lambda k: 2),
+        (8, lambda k: 3 - k // 2, lambda k: 1 - k % 2),
+        (14, lambda k: 5 - k // 3, lambda k: 2 - k % 3),
+        (18, lambda k: 3 - k, lambda k: 2),
+        (26, lambda k: 7 - k // 4, lambda k: 3 - k % 4),
+        (32, lambda k: 5 - k, lambda k: 3),
     )
     first = 0
     pair, group = jnp.int32(0), jnp.int32(0)
-    for last, _, pair_of, group_of in table:
+    for last, pair_of, group_of in table:
         inside = jnp.logical_and(index >= first, index < last)
         pair = jnp.where(inside, pair_of(index - first), pair)
         group = jnp.where(inside, group_of(index - first), group)
@@ -73,7 +74,7 @@
     img_in, txt_in, ids_in, scale_ref, bias_ref,
     img_out, txt_out, loss_out,
     img_raw, txt_raw, ids_raw, scale_raw, bias_raw,
-    img, txt, ids, dimg, swap, dtxt, even, odd, kept, sent, sent_s, got, got_s, loss_tile, loss_got,
+    img, txt, ids, dimg, swap, dtxt, even, odd, sent, sent_s, got, got_s, loss_tile, loss_got,
     load_sem, send_sem, recv_sem,
 ):
     x, core = lax.axis_index("x"), lax.axis_index("core")
@@ -114,6 +115,9 @@
     for axis, here in (("x", x), ("y", y), ("z", z)):
         for step in (1, 2, 3):
             peers.append({axis: lax.rem(here + step, 4)})
+    for step in (1, 3):
+        peers.append({"x": lax.rem(x + step, 4), "z": z_img})
+        peers.append({"y": lax.rem(y + step, 4), "z": z_txt})
     for peer in peers:
         pl.semaphore_signal(barrier, inc=1, device_id=peer, device_id_type=MESH)
 
@@ -141,7 +145,8 @@
             "plus_par": ((0, 1), (3, 1), plus[ring]),
             "minus_par": ((0, 1), (1, 1), minus[ring]),
             "plus_far": ((3, 0), (2, 0), plus[ring]),
-            "minus_far": ((1, 1), (2, 1), minus[ring]),
+            "minus_far": ((1, 0), (2, 0), minus[ring]),
+            "z_far": ((2, 0), (2, 1), across[ring]),
         }[name]
         src, dst = AT[src], AT[dst]
         if kind == "ids":
@@ -214,47 +219,57 @@
     dimg[...] = jnp.zeros_like(dimg)
     dtxt[...] = jnp.zeros_like(dtxt)
     loss_tile[0] = jnp.zeros_like(loss_tile[0])
-    for part in HALVES:
-        for kind in ("img", "txt"):
-            come(kind, "z", part)
-            go(kind, "plus_par", part)
-            go(kind, "minus_par", part)
-        for kind in ("img", "txt"):
-            come(kind, "plus_own", part)
-            go(kind, "plus_far", part)
+    for kind in ("img", "txt"):
+        come(kind, "plus_own", 0)
+        go(kind, "plus_far", 0)
+    for kind in ("img", "txt"):
+        come(kind, "z", 0)
+        go(kind, "plus_par", 0)
+        go(kind, "minus_par", 0)
+    for kind in ("img", "txt"):
+        come(kind, "minus_own", 0)
+        come(kind, "minus_own", 1)
+        go(kind, "minus_far", 1)
+    give((1, 0))
+    for kind in ("img", "txt"):
+        come(kind, "z", 1)
+        go(kind, "plus_par", 1)
+        go(kind, "minus_par", 1)
     give((0, 1))
+    for kind in ("img", "txt"):
+        come(kind, "plus_own", 1)
     give((3, 0))
-    for part in HALVES:
-        come("img", "minus_own", part)
-        come("txt", "minus_own", part)
-    give((1, 0))
-
     for place in range(4):
         share(place).wait_recv()
 
-    def early(index, carry):
-        kept[index] = make_coeff(3 - index // 2, 1 - lax.rem(index, 2))
-        return carry
-
-    lax.fori_loop(0, 8, early, 0)
-    for part in HALVES:
+    def far_on():
         for kind in ("img", "txt"):
-            come(kind, "minus_par", part)
-            go(kind, "minus_far", part)
-    give((1, 1))
-    for part in HALVES:
-        come("img", "plus_par", part)
-        come("txt", "plus_par", part)
-    give((3, 1))
-    for name, place in (("plus_far", (2, 0)), ("minus_far", (2, 1))):
+            come(kind, "plus_far", 0)
+            go(kind, "z_far", 0)
+        for kind in ("img", "txt"):
+            come(kind, "minus_far", 1)
+            go(kind, "z_far", 1)
+        give((2, 0))
+
+    def partners_here():
+        for name, place in (("minus_par", (1, 1)), ("plus_par", (3, 1))):
+            for part in HALVES:
+                come("img", name, part)
+            give(place)
+        for name in ("minus_par", "plus_par"):
+            for part in HALVES:
+                come("txt", name, part)
+        for place in ((1, 1), (3, 1)):
+            share(AT[place]).wait_recv()
+
+    def far_here():
         for part in HALVES:
-            come("img", name, part)
-        give(place)
-    for name in ("plus_far", "minus_far"):
+            come("img", "z_far", part)
+        give((2, 1))
         for part in HALVES:
-            come("txt", name, part)
-    for place in range(4, N_PLACE):
-        share(place).wait_recv()
+            come("txt", "z_far", part)
+        for place in ((2, 0), (2, 1)):
+            share(AT[place]).wait_recv()
 
     eye = lax.broadcasted_iota(jnp.int32, (HALF, ROWS), 0) == lax.broadcasted_iota(
         jnp.int32, (HALF, ROWS), 1
@@ -278,6 +293,8 @@
         ring = "img" if kind == "dimg" else "txt"
         if name == "z":
             return across[ring]
+        if name == "relay_minus":
+            return {**minus[ring], **across[ring]}
         return plus[ring] if name.endswith("plus") else minus[ring]
 
     def values(kind, name, part):
@@ -358,13 +375,30 @@
     def loss_swap():
         return copy(FLOWS["loss_core"], loss_tile.at[0], loss_got.at[0, 0], other)
 
+    def near_dtxt(part):
+        send("dtxt", "near_plus", (1, 1), part)
+        send("dtxt", "near_minus", (3, 0), part)
+
+    def two_back(place):
+        pass_back(place)
+        pass_back(place - 1)
+
+    def sixth_back():
+        pass_back(6)
+        near_dtxt(0)
+
+    def third_back():
+        two_back(3)
+        far_dimg()
+
     events = {
-        1: lambda: pass_back(7),
-        3: lambda: pass_back(6),
-        5: far_dimg,
-        6: far_dtxt,
-        8: lambda: pass_back(5),
-        9: lambda: pass_back(4),
+        0: far_on,
+        2: partners_here,
+        7: far_here,
+        10: lambda: pass_back(7),
+        12: sixth_back,
+        13: lambda: two_back(5),
+        14: third_back,
     }
 
     def make(index, buffer):
@@ -384,57 +418,50 @@
             pl.when(index == moment)(event)
         return carry
 
-    lax.fori_loop(0, 11, step, 0)
-    make(jnp.int32(23), odd)
+    lax.fori_loop(0, 15, step, 0)
+    make(jnp.int32(31), odd)
     launch(loss_swap)
-    use(jnp.int32(22), even)
-    use(jnp.int32(23), odd)
-
-    merge((3, 1))
-    relay("dimg", "minus", (3, 1))
+    use(jnp.int32(30), even)
+    use(jnp.int32(31), odd)
+    two_back(1)
+
+    far_dtxt()
+    loss_swap().wait_recv()
+    loss_tile[1] = loss_tile[0] + loss_got[0, 0]
+    loss_send("z", z, 1)
     merge((1, 1))
     send_all("dimg", "near_plus", (1, 1))
-    loss_swap().wait_recv()
-    loss_tile[1] = loss_tile[0] + loss_got[0, 0]
-    loss_send("y", y, 1)
-    relay("dtxt", "minus", (3, 1))
-    send_all("dtxt", "near_plus", (1, 1))
-
-    def late(index, carry):
-        use_coeff(kept[2 * index], 3 - index, 1)
-        use_coeff(kept[2 * index + 1], 3 - index, 0)
-        give_back(3 - index).start()
-        return carry
-
-    lax.fori_loop(0, 2, late, 0)
-    loss_take("y", y, 1)
-    loss_send("z", z, 2)
-    lax.fori_loop(2, 4, late, 0)
-    for place in range(4):
-        started.append(lambda place=place: give_back(place))
-
-    relay("dtxt", "plus", (1, 0))
-    send_all("dtxt", "near_minus", (3, 0))
     merge((3, 0))
     send_all("dimg", "near_minus", (3, 0))
+    merge((3, 1))
     merge((1, 0))
+    merge((0, 1))
+    merge((0, 0))
+    loss_take("z", z, 1)
+    loss_send("x", x, 2)
+    add("dtxt", "near_plus", (0, 1), 0)
+    send("dtxt", "z", (0, 1), 0)
+    relay("dimg", "minus", (3, 1))
     relay("dimg", "plus", (1, 0))
-    merge((0, 1))
-    for kind in ("dimg", "dtxt"):
-        for part in HALVES:
-            add(kind, "near_plus", (0, 1), part)
-    loss_take("z", z, 2)
-    loss_send("x", x, 3)
-    for kind in ("dimg", "dtxt"):
-        for part in HALVES:
-            add(kind, "relay_minus", (0, 1), part)
-            send(kind, "z", (0, 1), part)
-    merge((0, 0))
-    for name in ("near_minus", "relay_plus"):
-        for kind in ("dtxt", "dimg"):
+    relay("dtxt", "minus", (3, 1))
+    relay("dtxt", "plus", (1, 0))
+    near_dtxt(1)
+    for part in HALVES:
+        add("dimg", "near_plus", (0, 1), part)
+        send("dimg", "z", (0, 1), part)
+    loss_take("x", x, 2)
+    loss_send("y", y, 3)
+    add("dtxt", "near_minus", (0, 0), 0)
+    for part in HALVES:
+        add("dimg", "near_minus", (0, 0), part)
+    add("dtxt", "near_plus", (0, 1), 1)
+    send("dtxt", "z", (0, 1), 1)
+    for name in ("relay_plus", "relay_minus"):
+        for kind in ("dimg", "dtxt"):
             for part in HALVES:
                 add(kind, name, (0, 0), part)
-    loss_take("x", x, 3)
+    add("dtxt", "near_minus", (0, 0), 1)
+    loss_take("y", y, 3)
     count = F32(ROWS * 128)
     loss_out[0] = jnp.sum(loss_tile[4]) / (count * count)
     for kind, source, out in (("dimg", img_raw, img_out), ("dtxt", txt_raw, txt_out)):
@@ -478,7 +505,6 @@
             pltpu.VMEM((8 * rows, width), F32),
             pltpu.VMEM((2 * rows, 2 * rows), BF16),
             pltpu.VMEM((2 * rows, 2 * rows), BF16),
-            pltpu.VMEM((8, 2 * rows, 2 * rows), BF16),
             pltpu.VMEM((28, HALF, width), jnp.int16),
             pltpu.VMEM((28, 8, rows), F32),
             pltpu.VMEM((28, HALF, width), jnp.int16),

time: 78.8 us -> 83.6 us (1.061)
  Pallas kernels: 72.2 us -> 77 us
    pallas_call x1, Pallas kernels: 72.2 us -> 77 us  [per_device(): pl.pallas_call(kernel, out_shape=(jax.ShapeDtypeStruct((rows, width), F32...]
where the time goes in v5:
time: 83.6 us; the launch traced here: 83.4 us
  Pallas kernels  77 us (92%)
  between operations  3.67 us (4%)
  local copies, waits for them, and re-layouts  2.8 us (3%)
    pallas_call x1, Pallas kernels, per_device(): pl.pallas_call(kernel, out_shape=(jax.ShapeDtypeStruct((rows, width), F32...  77 us
    unnamed x4, local copies, waits for them, and re-layouts  2.8 us

profile of v5, /device:TPU:0, one launch (start us, length us, event | category | flops | bytes accessed | tf_op | source)
XLA Modules:
  0.0 83.4 jit_solution(12271686635424078534)
XLA Ops:
  1.9 77.0 %pair_grads.1 = (f32[128,1152]{1,0:T(8,128)}, f32[128,1152]{1,0:T(8,128)}, f32[1]{0:T(128)}) custom-call(bf16[128,1152]{1,0:T(8,128)(2,1)} %img_in.1, bf16[128,1152]{1,0:T(8,128)(2,1)} %txt_in.1, s32[1,128]{1,0:T(1,128)} %bitcast.1, f32[1]{0:T(128)S(6)} %copy.11.scale_ref, f32[1]{0:T(128)S(6)} %copy.12.bias_ref), custom_call_target="tpu_custom_call" | custom-call | tf_op jit(solution)/shard_map/pair_grads/pallas_call | solution.py:485
  78.9 0.0 copy-start
  78.9 2.0 %copy.13 = f32[128,1152]{1,0:T(8,128)} copy(f32[128,1152]{1,0:T(8,128)} %get-tuple-element.6) | data formatting | bytes 1179648
  80.9 0.0 copy-done
  80.9 0.8 copy.14
Async XLA Ops:
  78.9 2.0 %copy-start = (f32[128,1152]{1,0:T(8,128)S(1)}, f32[128,1152]{1,0:T(8,128)}, u32[]{:S(2)}) copy-start(f32[128,1152]{1,0:T(8,128)} %get-tuple-element.7) | copy-start | bytes 1769476

commit v6 on v5

v6 whole, which is shorter than its diff:
```python
import jax
import jax.numpy as jnp
from jax import lax
from jax.experimental import pallas as pl
from jax.experimental.pallas import tpu as pltpu
from jax.sharding import Mesh
from jax.sharding import PartitionSpec as P

AXES = ("x", "core", "y", "z")
MESH = pl.DeviceIdType.MESH
EPSILON = 1e-06
ROWS = 128
WIDTH = 1152
BF16 = jnp.bfloat16
F32 = jnp.float32

PLACES = (0b000, 0b001, 0b010, 0b100, 0b011, 0b101, 0b110, 0b111)
AT = {place: index for index, place in enumerate(PLACES)}
N_PLACE = len(PLACES)
THIRDS = (0, 1, 2)
ORDER = ((0, 1, 2), (1, 2, 0), (2, 0, 1))


def level(third, place):
    return max((n for n, axis in enumerate(ORDER[third]) if place >> axis & 1), default=-1)


def onward(third, place):
    return [place | 1 << axis for axis in ORDER[third][level(third, place) + 1 :]]


FLOWS = {}
for place in PLACES[1:]:
    FLOWS["ids", place] = len(FLOWS)
    for kind in ("img", "txt", "dimg", "dimg_s", "dtxt", "dtxt_s"):
        for third in THIRDS:
            FLOWS[kind, third, place] = len(FLOWS)
for place in range(N_PLACE):
    FLOWS["share", place] = len(FLOWS)
for place in range(N_PLACE):
    FLOWS["swap", place] = len(FLOWS)
FLOWS["loss_core"] = len(FLOWS)
for axis in ("x", "y", "z"):
    for step in (1, 2, 3):
        FLOWS["loss", axis, step] = len(FLOWS)
N_FLOW = len(FLOWS)


def normalize(values):
    wide = values.astype(F32)
    recip = lax.rsqrt(jnp.sum(wide * wide, axis=1, keepdims=True) + EPSILON)
    return (wide * recip, recip)


def project_back(unit, recip, grad):
    return recip * (grad - unit * jnp.sum(unit * grad, axis=1, keepdims=True))


def tile_at(index):
    table = (
        (8, lambda k: 3 - k // 2, lambda k: 1 - k % 2),
        (16, lambda k: 7 - k // 4, lambda k: 3 - k % 4),
        (22, lambda k: 5 - k, lambda k: 3),
        (28, lambda k: 5 - k // 3, lambda k: 2 - k % 3),
        (32, lambda k: 3 - k, lambda k: 2),
    )
    first = 0
    pair, group = jnp.int32(0), jnp.int32(0)
    for last, pair_of, group_of in table:
        inside = jnp.logical_and(index >= first, index < last)
        pair = jnp.where(inside, pair_of(index - first), pair)
        group = jnp.where(inside, group_of(index - first), group)
        first = last
    return pair, group


def kernel(
    img_in, txt_in, ids_in, scale_ref, bias_ref,
    img_out, txt_out, loss_out,
    img_raw, txt_raw, ids_raw, scale_raw, bias_raw,
    img, txt, ids, dimg, swap, dtxt, even, odd, sent, sent_s, got, got_s, loss_tile, loss_got,
    load_sem, send_sem, recv_sem,
):
    x, core = lax.axis_index("x"), lax.axis_index("core")
    y, z = lax.axis_index("y"), lax.axis_index("z")
    other = {"core": 1 - core}
    here = {"x": x, "y": y, "z": z}
    partner = {
        "img": [{axis: at + 1 - 2 * lax.rem(at, 2)} for axis, at in here.items()],
        "txt": [{axis: 3 - at} for axis, at in here.items()],
    }
    partner["dimg"] = partner["img"]
    partner["dtxt"] = partner["ids"] = partner["txt"]

    loads = [
        pltpu.make_async_copy(src, dst, load_sem.at[number])
        for number, (src, dst) in enumerate(
            (
                (img_in, img_raw), (txt_in, txt_raw), (ids_in, ids_raw),
                (scale_ref, scale_raw), (bias_ref, bias_raw),
            )
        )
    ]
    for load in loads:
        load.start()

    started = []

    def copy(flow, src, dst, device):
        return pltpu.make_async_remote_copy(
            src_ref=src, dst_ref=dst, send_sem=send_sem.at[flow], recv_sem=recv_sem.at[flow],
            device_id=device, device_id_type=MESH,
        )

    def launch(make):
        make().start()
        started.append(make)

    barrier = pltpu.get_barrier_semaphore()
    peers = [other]
    for axis, here in (("x", x), ("y", y), ("z", z)):
        for step in (1, 2, 3):
            peers.append({axis: lax.rem(here + step, 4)})
    for peer in peers:
        pl.semaphore_signal(barrier, inc=1, device_id=peer, device_id_type=MESH)

    def img_rows(place, which):
        return pl.ds((2 * place + which) * ROWS, ROWS)

    def rows(place):
        return pl.ds(place * ROWS, ROWS)

    for load in loads:
        load.wait()
    img[img_rows(0, 0), :] = normalize(img_raw[...])[0].astype(BF16)
    txt[rows(0), :] = normalize(txt_raw[...])[0].astype(BF16)
    ids[0] = jnp.broadcast_to(ids_raw[...], (8, ROWS)) + x * (16 * ROWS)
    scale = scale_raw[0]
    bias = bias_raw[0]
    pl.semaphore_wait(barrier, len(peers))

    def columns(third):
        return pl.ds(third * (WIDTH // 3), WIDTH // 3)

    def route(kind, third, place):
        return partner[kind][ORDER[third][level(third, place)]]

    def before(third, place):
        return place ^ 1 << ORDER[third][level(third, place)]

    def gather(kind, third, place):
        src, dst = AT[before(third, place)], AT[place]
        device = route(kind, third, place)
        if kind == "ids":
            return copy(FLOWS[kind, place], ids.at[src], ids.at[dst], device)
        ref, every = (img, 2) if kind == "img" else (txt, 1)
        return copy(
            FLOWS[kind, third, place],
            ref.at[pl.ds(src * every * ROWS, ROWS), columns(third)],
            ref.at[pl.ds(dst * every * ROWS, ROWS), columns(third)],
            device,
        )

    def share(place):
        return copy(
            FLOWS["share", place], img.at[img_rows(place, 0), :], img.at[img_rows(place, 1), :], other
        )

    def go(kind, third, place):
        launch(lambda: gather(kind, third, place))
        if kind == "txt" and third == 0:
            launch(lambda: gather("ids", third, place))

    def give(place):
        launch(lambda: share(AT[place]))

    def come(third, place):
        for kind in ("img", "txt"):
            gather(kind, third, place).wait_recv()
            if kind == "txt" and third == 0:
                gather("ids", third, place).wait_recv()
            for later in onward(third, place):
                go(kind, third, later)

    row_iota = lax.broadcasted_iota(jnp.int32, (2 * ROWS, 1), 0)

    def span(number):
        return pl.ds(pl.multiple_of(number * (2 * ROWS), 2 * ROWS), 2 * ROWS)

    def make_coeff(pair, group):
        logits = scale * lax.dot_general(
            img[span(pair), :], txt[span(group), :], (((1,), (1,)), ((), ())),
            preferred_element_type=F32,
        ) + bias
        with_y = jnp.logical_or(pair == AT[0b010], pair == AT[0b110])
        with_z = jnp.logical_or(pair == AT[0b100], pair == AT[0b110])
        owner = (
            x * 16
            + jnp.where(with_y, partner["img"][1]["y"], y) * 4
            + jnp.where(with_z, partner["img"][2]["z"], z)
        ) * ROWS
        same_x = jnp.logical_or(pair == 0, jnp.logical_or(with_y, with_z))
        valid = jnp.logical_and(same_x, row_iota < ROWS)
        row_ids = jnp.where(valid, owner + row_iota, -1)
        column_ids = jnp.concatenate(
            [ids[2 * group, 0:1, :], ids[2 * group + 1, 0:1, :]], axis=1
        )
        same = row_ids == column_ids
        logits = jnp.where(same, -logits, logits)
        power = jnp.exp(logits)
        one_plus = 1.0 + power
        recip = 1.0 / one_plus
        sigmoid = power * recip
        softplus = jnp.log(one_plus) + (power - (one_plus - 1.0)) * recip
        folded = jnp.sum(softplus.reshape(32, 8, 256), axis=0)
        loss_tile[0] += folded[:, :128] + folded[:, 128:]
        return jnp.where(same, -sigmoid, sigmoid).astype(BF16)

    def use_coeff(half, pair, group):
        here, there = span(pair), span(group)
        dimg[here, :] += jnp.dot(half, txt[there, :], preferred_element_type=F32)
        dtxt[there, :] += lax.dot_general(
            half, img[here, :], (((0,), (0,)), ((), ())), preferred_element_type=F32
        )

    for turn in range(3):
        for axis in range(3):
            for kind in ("img", "txt"):
                go(kind, (axis - turn) % 3, 1 << axis)
    give(0)
    dimg[...] = jnp.zeros_like(dimg)
    dtxt[...] = jnp.zeros_like(dtxt)
    loss_tile[0] = jnp.zeros_like(loss_tile[0])
    for turn in range(3):
        for axis in range(3):
            come((axis - turn) % 3, 1 << axis)
    for axis in range(3):
        give(1 << axis)
    for place in range(4):
        share(place).wait_recv()

    def firsts(third):
        return 1 << ORDER[third][0] | 1 << ORDER[third][1]

    def pass_on():
        for third in THIRDS:
            come(third, firsts(third))

    def all_here():
        for place in (0b111, 0b110, 0b101, 0b011):
            for third in THIRDS:
                if place != firsts(third):
                    come(third, place)
            give(place)
        for place in (0b111, 0b110, 0b101, 0b011):
            share(AT[place]).wait_recv()

    eye = lax.broadcasted_iota(jnp.int32, (ROWS, ROWS), 0) == lax.broadcasted_iota(
        jnp.int32, (ROWS, ROWS), 1
    )

    def give_back(place):
        return copy(
            FLOWS["swap", 0] + place, dimg.at[img_rows(place, 1), :], swap.at[rows(place), :], other
        )

    def slot(kind, third, place):
        return ((place - 1) * 3 + third) * 2 + (kind == "dtxt")

    def sum_ref(kind, third, place):
        if kind == "dimg":
            return dimg.at[pl.ds(AT[place] * 2 * ROWS, ROWS), columns(third)]
        return dtxt.at[pl.ds(AT[place] * ROWS, ROWS), columns(third)]

    def values(kind, third, place):
        s = slot(kind, third, place)
        return copy(FLOWS[kind, third, place], sent.at[s], got.at[s], route(kind, third, place))

    def units(kind, third, place):
        s = slot(kind, third, place)
        return copy(
            FLOWS[kind + "_s", third, place], sent_s.at[s], got_s.at[s], route(kind, third, place)
        )

    def send(kind, third, place):
        for child in onward(third, place):
            add(kind, third, child)
        ref = sum_ref(kind, third, place)
        s = slot(kind, third, place)
        top = jnp.maximum(jnp.max(jnp.abs(ref[...]), axis=1, keepdims=True), 1e-30)
        across_lanes = jnp.sum(jnp.where(eye, top * (1.0 / 32767.0), 0.0), axis=0, keepdims=True)
        sent_s[s] = jnp.broadcast_to(across_lanes, (8, ROWS))
        sent[s] = jnp.round(ref[...] * (32767.0 / top)).astype(jnp.int32).astype(jnp.int16)
        launch(lambda: values(kind, third, place))
        launch(lambda: units(kind, third, place))

    def take(kind, third, place):
        s = slot(kind, third, place)
        values(kind, third, place).wait_recv()
        units(kind, third, place).wait_recv()
        unit = jnp.sum(jnp.where(eye, got_s[s, 0:1, :], 0.0), axis=1, keepdims=True)
        return got[s].astype(jnp.int32).astype(F32) * unit

    def add(kind, third, place):
        sum_ref(kind, third, before(third, place))[...] += take(kind, third, place)

    def merge(place):
        give_back(AT[place]).wait_recv()
        dimg[img_rows(AT[place], 0), :] += swap[rows(AT[place]), :]

    def send_now(kind, place):
        for third in THIRDS:
            if not onward(third, place):
                send(kind, third, place)

    def pass_back(place):
        launch(lambda: give_back(place))

    def loss_send(axis, here, number):
        loss_got[number, here] = loss_tile[number]
        for stride in (1, 2, 3):
            launch(
                lambda stride=stride: copy(
                    FLOWS["loss", axis, stride], loss_tile.at[number], loss_got.at[number, here],
                    {axis: lax.rem(here + stride, 4)},
                )
            )

    def loss_take(axis, here, number):
        for stride in (1, 2, 3):
            source = lax.rem(here + 4 - stride, 4)
            copy(
                FLOWS["loss", axis, stride], loss_tile.at[number], loss_got.at[number, source],
                {axis: lax.rem(here + stride, 4)},
            ).wait_recv()
        loss_tile[number + 1] = (loss_got[number, 0] + loss_got[number, 1]) + (
            loss_got[number, 2] + loss_got[number, 3]
        )

    def loss_swap():
        return copy(FLOWS["loss_core"], loss_tile.at[0], loss_got.at[0, 0], other)

    def two_back(place):
        pass_back(place)
        pass_back(place - 1)

    def after_7():
        pass_back(6)
        merge(0b111)
        send_now("dimg", 0b111)

    def after_9():
        merge(0b110)
        send_now("dimg", 0b110)

    def after_10():
        send_now("dtxt", 0b111)
        send_now("dtxt", 0b110)

    def after_13():
        pass_back(4)
        for axis in range(3):
            send_now("dtxt", 1 << axis)

    def after_14():
        two_back(3)
        merge(0b101)
        send_now("dimg", 0b101)

    events = {
        0: pass_on,
        2: all_here,
        5: lambda: pass_back(7),
        7: after_7,
        9: after_9,
        10: after_10,
        12: lambda: pass_back(5),
        13: after_13,
        14: after_14,
    }

    def make(index, buffer):
        buffer[...] = make_coeff(*tile_at(index))

    def use(index, buffer):
        use_coeff(buffer[...], *tile_at(index))

    make(jnp.int32(0), even)

    def step(index, carry):
        make(2 * index + 1, odd)
        use(2 * index, even)
        make(2 * index + 2, even)
        use(2 * index + 1, odd)
        for moment, event in events.items():
            pl.when(index == moment)(event)
        return carry

    lax.fori_loop(0, 15, step, 0)
    make(jnp.int32(31), odd)
    launch(loss_swap)
    use(jnp.int32(30), even)
    use(jnp.int32(31), odd)
    two_back(1)

    send_now("dtxt", 0b101)
    send_now("dtxt", 0b011)
    merge(0b011)
    send_now("dimg", 0b011)
    loss_swap().wait_recv()
    loss_tile[1] = loss_tile[0] + loss_got[0, 0]
    loss_send("z", z, 1)
    for third in THIRDS:
        for kind in ("dimg", "dtxt"):
            send(kind, third, firsts(third))
    for axis in range(3):
        merge(1 << axis)
        send_now("dimg", 1 << axis)
    merge(0)
    loss_take("z", z, 1)
    loss_send("x", x, 2)
    for third in THIRDS:
        for kind in ("dtxt", "dimg"):
            send(kind, third, 1 << ORDER[third][1])
    loss_take("x", x, 2)
    loss_send("y", y, 3)
    for third in THIRDS:
        for kind in ("dtxt", "dimg"):
            send(kind, third, 1 << ORDER[third][0])
    for turn in (2, 1, 0):
        for third in THIRDS:
            for kind in ("dtxt", "dimg"):
                add(kind, third, 1 << ORDER[third][turn])
    loss_take("y", y, 3)
    count = F32(ROWS * 128)
    loss_out[0] = jnp.sum(loss_tile[4]) / (count * count)
    for kind, source, out in (("dtxt", txt_raw, txt_out), ("dimg", img_raw, img_out)):
        own = pl.ds(0, ROWS)
        grad = scale * (dimg if kind == "dimg" else dtxt)[own, :]
        unit, recip = normalize(source[...])
        out[...] = project_back(unit, recip, grad)

    for make in started:
        make().wait_send()


def per_device(images, texts, lang_order, position, logit_scale, logit_bias):
    rows, width = images.shape
    ids = lang_order.reshape(1, rows)
    whole = pl.BlockSpec(memory_space=pl.ANY)
    vmem = pl.BlockSpec(memory_space=pltpu.VMEM)
    smem = pl.BlockSpec(memory_space=pltpu.SMEM)
    return pl.pallas_call(
        kernel,
        out_shape=(
            jax.ShapeDtypeStruct((rows, width), F32),
            jax.ShapeDtypeStruct((rows, width), F32),
            jax.ShapeDtypeStruct((1,), F32),
        ),
        in_specs=[whole] * 5,
        out_specs=(vmem, vmem, smem),
        scratch_shapes=[
            pltpu.VMEM((rows, width), BF16),
            pltpu.VMEM((rows, width), BF16),
            pltpu.VMEM((1, rows), jnp.int32),
            pltpu.SMEM((1,), F32),
            pltpu.SMEM((1,), F32),
            pltpu.VMEM((16 * rows, width), BF16),
            pltpu.VMEM((8 * rows, width), BF16),
            pltpu.VMEM((8, 8, rows), jnp.int32),
            pltpu.VMEM((16 * rows, width), F32),
            pltpu.VMEM((8 * rows, width), F32),
            pltpu.VMEM((8 * rows, width), F32),
            pltpu.VMEM((2 * rows, 2 * rows), BF16),
            pltpu.VMEM((2 * rows, 2 * rows), BF16),
            pltpu.VMEM((42, rows, width // 3), jnp.int16),
            pltpu.VMEM((42, 8, rows), F32),
            pltpu.VMEM((42, rows, width // 3), jnp.int16),
            pltpu.VMEM((42, 8, rows), F32),
            pltpu.VMEM((5, 8, 128), F32),
            pltpu.VMEM((4, 4, 8, 128), F32),
            pltpu.SemaphoreType.DMA((5,)),
            pltpu.SemaphoreType.DMA((N_FLOW,)),
            pltpu.SemaphoreType.DMA((N_FLOW,)),
        ],
        compiler_params=pltpu.CompilerParams(
            collective_id=0, has_side_effects=True, vmem_limit_bytes=62 * 1024 * 1024
        ),
        name="pair_grads",
    )(images, texts, ids, logit_scale, logit_bias)


def solution(mesh):
    finer = Mesh(mesh.devices.reshape(4, 2, 4, 4), AXES)
    return jax.shard_map(
        per_device,
        mesh=finer,
        in_specs=(P(AXES, None), P(AXES, None), P(AXES), P(AXES), P(), P()),
        out_specs=(P(AXES, None), P(AXES, None), P()),
        check_vma=False,
    )
```

time: 83.6 us -> 79 us (0.945)
  Pallas kernels: 77 us -> 71.9 us
    pallas_call x1, Pallas kernels: 77 us -> 71.9 us  [per_device(): pl.pallas_call(kernel, out_shape=(jax.ShapeDtypeStruct((rows, width), F32...]
where the time goes in v6:
time: 79 us; the launch traced here: 78.4 us
  Pallas kernels  71.9 us (91%)
  between operations  3.67 us (5%)
  local copies, waits for them, and re-layouts  2.8 us (4%)
    pallas_call x1, Pallas kernels, per_device(): pl.pallas_call(kernel, out_shape=(jax.ShapeDtypeStruct((rows, width), F32...  71.9 us
    unnamed x4, local copies, waits for them, and re-layouts  2.8 us

profile of v6, /device:TPU:0, one launch (start us, length us, event | category | flops | bytes accessed | tf_op | source)
XLA Modules:
  0.0 78.4 jit_solution(4653783149568049738)
XLA Ops:
  1.9 71.9 %pair_grads.1 = (f32[128,1152]{1,0:T(8,128)}, f32[128,1152]{1,0:T(8,128)}, f32[1]{0:T(128)}) custom-call(bf16[128,1152]{1,0:T(8,128)(2,1)} %img_in.1, bf16[128,1152]{1,0:T(8,128)(2,1)} %txt_in.1, s32[1,128]{1,0:T(1,128)} %bitcast.1, f32[1]{0:T(128)S(6)} %copy.11.scale_ref, f32[1]{0:T(128)S(6)} %copy.12.bias_ref), custom_call_target="tpu_custom_call" | custom-call | tf_op jit(solution)/shard_map/pair_grads/pallas_call | solution.py:453
  73.9 0.0 copy-start
  73.9 2.0 %copy.13 = f32[128,1152]{1,0:T(8,128)} copy(f32[128,1152]{1,0:T(8,128)} %get-tuple-element.6) | data formatting | bytes 1179648
  75.8 0.0 copy-done
  75.8 0.8 %copy.14 = f32[128,1152]{1,0:T(8,128)} copy(f32[128,1152]{1,0:T(8,128)S(1)} %copy-done) | data formatting | bytes 1179648
Async XLA Ops:
  73.9 2.0 %copy-start = (f32[128,1152]{1,0:T(8,128)S(1)}, f32[128,1152]{1,0:T(8,128)}, u32[]{:S(2)}) copy-start(f32[128,1152]{1,0:T(8,128)} %get-tuple-element.7) | copy-start | bytes 1769476

commit v7 on v6

--- a/solution.py
+++ b/solution.py
@@ -58,11 +58,12 @@
 
 def tile_at(index):
     table = (
-        (8, lambda k: 3 - k // 2, lambda k: 1 - k % 2),
-        (16, lambda k: 7 - k // 4, lambda k: 3 - k % 4),
-        (22, lambda k: 5 - k, lambda k: 3),
-        (28, lambda k: 5 - k // 3, lambda k: 2 - k % 3),
-        (32, lambda k: 3 - k, lambda k: 2),
+        (4, lambda k: 1 - k // 2, lambda k: 1 - k % 2),
+        (6, lambda k: 2, lambda k: 1 - k),
+        (7, lambda k: 2, lambda k: 2),
+        (11, lambda k: 3, lambda k: 3 - k),
+        (14, lambda k: 2 - k, lambda k: 3),
+        (16, lambda k: 1 - k, lambda k: 2),
     )
     first = 0
     pair, group = jnp.int32(0), jnp.int32(0)
@@ -182,26 +183,33 @@
             for later in onward(third, place):
                 go(kind, third, later)
 
-    row_iota = lax.broadcasted_iota(jnp.int32, (2 * ROWS, 1), 0)
+    tall = 4 * ROWS
+    row_iota = lax.broadcasted_iota(jnp.int32, (tall, 1), 0)
 
     def span(number):
         return pl.ds(pl.multiple_of(number * (2 * ROWS), 2 * ROWS), 2 * ROWS)
 
+    def tall_span(number):
+        return pl.ds(pl.multiple_of(number * tall, tall), tall)
+
     def make_coeff(pair, group):
         logits = scale * lax.dot_general(
-            img[span(pair), :], txt[span(group), :], (((1,), (1,)), ((), ())),
+            img[tall_span(pair), :], txt[span(group), :], (((1,), (1,)), ((), ())),
             preferred_element_type=F32,
         ) + bias
-        with_y = jnp.logical_or(pair == AT[0b010], pair == AT[0b110])
-        with_z = jnp.logical_or(pair == AT[0b100], pair == AT[0b110])
+        lower = row_iota < 2 * ROWS
+        place_at = 2 * pair + jnp.where(lower, 0, 1)
+        with_y = jnp.logical_or(place_at == AT[0b010], place_at == AT[0b110])
+        with_z = jnp.logical_or(place_at == AT[0b100], place_at == AT[0b110])
         owner = (
             x * 16
             + jnp.where(with_y, partner["img"][1]["y"], y) * 4
             + jnp.where(with_z, partner["img"][2]["z"], z)
         ) * ROWS
-        same_x = jnp.logical_or(pair == 0, jnp.logical_or(with_y, with_z))
-        valid = jnp.logical_and(same_x, row_iota < ROWS)
-        row_ids = jnp.where(valid, owner + row_iota, -1)
+        within = row_iota - jnp.where(lower, 0, 2 * ROWS)
+        same_x = jnp.logical_or(place_at == 0, jnp.logical_or(with_y, with_z))
+        valid = jnp.logical_and(same_x, within < ROWS)
+        row_ids = jnp.where(valid, owner + within, -1)
         column_ids = jnp.concatenate(
             [ids[2 * group, 0:1, :], ids[2 * group + 1, 0:1, :]], axis=1
         )
@@ -211,13 +219,15 @@
         one_plus = 1.0 + power
         recip = 1.0 / one_plus
         sigmoid = power * recip
-        softplus = jnp.log(one_plus) + (power - (one_plus - 1.0)) * recip
+        lost = (power - (one_plus - 1.0)) * recip
+        half = tall // 2
+        softplus = jnp.log(one_plus[:half] * one_plus[half:]) + (lost[:half] + lost[half:])
         folded = jnp.sum(softplus.reshape(32, 8, 256), axis=0)
         loss_tile[0] += folded[:, :128] + folded[:, 128:]
         return jnp.where(same, -sigmoid, sigmoid).astype(BF16)
 
     def use_coeff(half, pair, group):
-        here, there = span(pair), span(group)
+        here, there = tall_span(pair), span(group)
         dimg[here, :] += jnp.dot(half, txt[there, :], preferred_element_type=F32)
         dtxt[there, :] += lax.dot_general(
             half, img[here, :], (((0,), (0,)), ((), ())), preferred_element_type=F32
@@ -246,13 +256,22 @@
         for third in THIRDS:
             come(third, firsts(third))
 
-    def all_here():
-        for place in (0b111, 0b110, 0b101, 0b011):
+    def partners_here():
+        for place in (0b011, 0b101):
             for third in THIRDS:
                 if place != firsts(third):
                     come(third, place)
             give(place)
-        for place in (0b111, 0b110, 0b101, 0b011):
+        for place in (0b011, 0b101):
+            share(AT[place]).wait_recv()
+
+    def all_here():
+        for place in (0b110, 0b111):
+            for third in THIRDS:
+                if place != firsts(third):
+                    come(third, place)
+            give(place)
+        for place in (0b110, 0b111):
             share(AT[place]).wait_recv()
 
     eye = lax.broadcasted_iota(jnp.int32, (ROWS, ROWS), 0) == lax.broadcasted_iota(
@@ -290,7 +309,7 @@
         top = jnp.maximum(jnp.max(jnp.abs(ref[...]), axis=1, keepdims=True), 1e-30)
         across_lanes = jnp.sum(jnp.where(eye, top * (1.0 / 32767.0), 0.0), axis=0, keepdims=True)
         sent_s[s] = jnp.broadcast_to(across_lanes, (8, ROWS))
-        sent[s] = jnp.round(ref[...] * (32767.0 / top)).astype(jnp.int32).astype(jnp.int16)
+        sent[s] = ((ref[...] * (32767.0 / top) + 32768.5).astype(jnp.int32) - 32768).astype(jnp.int16)
         launch(lambda: values(kind, third, place))
         launch(lambda: units(kind, third, place))
 
@@ -344,39 +363,40 @@
         pass_back(place)
         pass_back(place - 1)
 
-    def after_7():
-        pass_back(6)
-        merge(0b111)
-        send_now("dimg", 0b111)
-
-    def after_9():
-        merge(0b110)
-        send_now("dimg", 0b110)
-
-    def after_10():
-        send_now("dtxt", 0b111)
-        send_now("dtxt", 0b110)
-
-    def after_13():
-        pass_back(4)
+    def far_dimg():
+        for place in (0b111, 0b110):
+            merge(place)
+            send_now("dimg", place)
+
+    def far_dtxt():
+        for place in (0b111, 0b110):
+            send_now("dtxt", place)
+
+    def near_dtxt():
         for axis in range(3):
             send_now("dtxt", 1 << axis)
 
-    def after_14():
-        two_back(3)
-        merge(0b101)
-        send_now("dimg", 0b101)
+    def partner_dimg():
+        for place in (0b101, 0b011):
+            merge(place)
+            send_now("dimg", place)
+
+    def far_back():
+        two_back(7)
+        near_dtxt()
+
+    def partner_out():
+        far_dtxt()
+        partner_dimg()
 
     events = {
         0: pass_on,
-        2: all_here,
-        5: lambda: pass_back(7),
-        7: after_7,
-        9: after_9,
-        10: after_10,
-        12: lambda: pass_back(5),
-        13: after_13,
-        14: after_14,
+        2: partners_here,
+        5: all_here,
+        10: far_back,
+        11: lambda: two_back(5),
+        12: far_dimg,
+        13: partner_out,
     }
 
     def make(index, buffer):
@@ -388,28 +408,29 @@
     make(jnp.int32(0), even)
 
     def step(index, carry):
-        make(2 * index + 1, odd)
-        use(2 * index, even)
-        make(2 * index + 2, even)
-        use(2 * index + 1, odd)
-        for moment, event in events.items():
-            pl.when(index == moment)(event)
+        for half, (new, old) in enumerate(((odd, even), (even, odd))):
+            make(2 * index + 1 + half, new)
+            use(2 * index + half, old)
+            for moment, event in events.items():
+                if moment % 2 == half:
+                    pl.when(index == moment // 2)(event)
         return carry
 
-    lax.fori_loop(0, 15, step, 0)
-    make(jnp.int32(31), odd)
+    lax.fori_loop(0, 7, step, 0)
+    make(jnp.int32(15), odd)
     launch(loss_swap)
-    use(jnp.int32(30), even)
-    use(jnp.int32(31), odd)
-    two_back(1)
-
-    send_now("dtxt", 0b101)
-    send_now("dtxt", 0b011)
-    merge(0b011)
-    send_now("dimg", 0b011)
+    use(jnp.int32(14), even)
+    two_back(3)
     loss_swap().wait_recv()
     loss_tile[1] = loss_tile[0] + loss_got[0, 0]
     loss_send("z", z, 1)
+    use(jnp.int32(15), odd)
+    two_back(1)
+
+    send_now("dtxt", 0b101)
+    send_now("dtxt", 0b011)
+    loss_take("z", z, 1)
+    loss_send("x", x, 2)
     for third in THIRDS:
         for kind in ("dimg", "dtxt"):
             send(kind, third, firsts(third))
@@ -417,13 +438,11 @@
         merge(1 << axis)
         send_now("dimg", 1 << axis)
     merge(0)
-    loss_take("z", z, 1)
-    loss_send("x", x, 2)
+    loss_take("x", x, 2)
+    loss_send("y", y, 3)
     for third in THIRDS:
         for kind in ("dtxt", "dimg"):
             send(kind, third, 1 << ORDER[third][1])
-    loss_take("x", x, 2)
-    loss_send("y", y, 3)
     for third in THIRDS:
         for kind in ("dtxt", "dimg"):
             send(kind, third, 1 << ORDER[third][0])
@@ -471,8 +490,8 @@
             pltpu.VMEM((16 * rows, width), F32),
             pltpu.VMEM((8 * rows, width), F32),
             pltpu.VMEM((8 * rows, width), F32),
-            pltpu.VMEM((2 * rows, 2 * rows), BF16),
-            pltpu.VMEM((2 * rows, 2 * rows), BF16),
+            pltpu.VMEM((4 * rows, 2 * rows), BF16),
+            pltpu.VMEM((4 * rows, 2 * rows), BF16),
             pltpu.VMEM((42, rows, width // 3), jnp.int16),
             pltpu.VMEM((42, 8, rows), F32),
             pltpu.VMEM((42, rows, width // 3), jnp.int16),

time: 79 us -> 76.1 us (0.963)
  Pallas kernels: 71.9 us -> 69.2 us
    pallas_call x1, Pallas kernels: 71.9 us -> 69.2 us  [per_device(): pl.pallas_call(kernel, out_shape=(jax.ShapeDtypeStruct((rows, width), F32...]
where the time goes in v7:
time: 76.1 us; the launch traced here: 75.7 us
  Pallas kernels  69.2 us (91%)
  between operations  3.67 us (5%)
  local copies, waits for them, and re-layouts  2.8 us (4%)
    pallas_call x1, Pallas kernels, per_device(): pl.pallas_call(kernel, out_shape=(jax.ShapeDtypeStruct((rows, width), F32...  69.2 us
    unnamed x4, local copies, waits for them, and re-layouts  2.8 us

profile of v7, /device:TPU:0, one launch (start us, length us, event | category | flops | bytes accessed | tf_op | source)
XLA Modules:
  0.0 75.7 jit_solution(4139839100847009378)
XLA Ops:
  1.9 69.2 %pair_grads.1 = (f32[128,1152]{1,0:T(8,128)}, f32[128,1152]{1,0:T(8,128)}, f32[1]{0:T(128)}) custom-call(bf16[128,1152]{1,0:T(8,128)(2,1)} %img_in.1, bf16[128,1152]{1,0:T(8,128)(2,1)} %txt_in.1, s32[1,128]{1,0:T(1,128)} %bitcast.1, f32[1]{0:T(128)S(6)} %copy.11.scale_ref, f32[1]{0:T(128)S(6)} %copy.12.bias_ref), custom_call_target="tpu_custom_call" | custom-call | tf_op jit(solution)/shard_map/pair_grads/pallas_call | solution.py:472
  71.2 0.0 copy-start
  71.2 2.0 %copy.13 = f32[128,1152]{1,0:T(8,128)} copy(f32[128,1152]{1,0:T(8,128)} %get-tuple-element.6) | data formatting | bytes 1179648
  73.2 0.0 copy-done
  73.2 0.8 %copy.14 = f32[128,1152]{1,0:T(8,128)} copy(f32[128,1152]{1,0:T(8,128)S(1)} %copy-done) | data formatting | bytes 1179648
Async XLA Ops:
  71.2 2.0 %copy-start = (f32[128,1152]{1,0:T(8,128)S(1)}, f32[128,1152]{1,0:T(8,128)}, u32[]{:S(2)}) copy-start(f32[128,1152]{1,0:T(8,128)} %get-tuple-element.7) | copy-start | bytes 1769476

commit v8 on v7

--- a/solution.py
+++ b/solution.py
@@ -31,8 +31,7 @@
 
 FLOWS = {}
 for place in PLACES[1:]:
-    FLOWS["ids", place] = len(FLOWS)
-    for kind in ("img", "txt", "dimg", "dimg_s", "dtxt", "dtxt_s"):
+    for kind in ("img", "txt", "dimg", "dtxt"):
         for third in THIRDS:
             FLOWS[kind, third, place] = len(FLOWS)
 for place in range(N_PLACE):
@@ -44,6 +43,7 @@
     for step in (1, 2, 3):
         FLOWS["loss", axis, step] = len(FLOWS)
 N_FLOW = len(FLOWS)
+SENT = ("img", "txt", "ids", "values", "units", "share", "swap", "loss_core", "loss")
 
 
 def normalize(values):
@@ -80,7 +80,7 @@
     img_out, txt_out, loss_out,
     img_raw, txt_raw, ids_raw, scale_raw, bias_raw,
     img, txt, ids, dimg, swap, dtxt, even, odd, sent, sent_s, got, got_s, loss_tile, loss_got,
-    load_sem, send_sem, recv_sem,
+    both, load_sem, send_sem, recv_sem,
 ):
     x, core = lax.axis_index("x"), lax.axis_index("core")
     y, z = lax.axis_index("y"), lax.axis_index("z")
@@ -105,17 +105,17 @@
     for load in loads:
         load.start()
 
-    started = []
-
-    def copy(flow, src, dst, device):
+    def copy(kind, flow, src, dst, device):
         return pltpu.make_async_remote_copy(
-            src_ref=src, dst_ref=dst, send_sem=send_sem.at[flow], recv_sem=recv_sem.at[flow],
-            device_id=device, device_id_type=MESH,
-        )
+            src_ref=src, dst_ref=dst, send_sem=send_sem.at[SENT.index(kind)],
+            recv_sem=recv_sem.at[flow], device_id=device, device_id_type=MESH,
+        )
+
+    def both_here(flow):
+        copy("ids", flow, both, both, other).wait_recv()
 
     def launch(make):
         make().start()
-        started.append(make)
 
     barrier = pltpu.get_barrier_semaphore()
     peers = [other]
@@ -153,9 +153,10 @@
         src, dst = AT[before(third, place)], AT[place]
         device = route(kind, third, place)
         if kind == "ids":
-            return copy(FLOWS[kind, place], ids.at[src], ids.at[dst], device)
+            return copy(kind, FLOWS["txt", 0, place], ids.at[src], ids.at[dst], device)
         ref, every = (img, 2) if kind == "img" else (txt, 1)
         return copy(
+            kind,
             FLOWS[kind, third, place],
             ref.at[pl.ds(src * every * ROWS, ROWS), columns(third)],
             ref.at[pl.ds(dst * every * ROWS, ROWS), columns(third)],
@@ -164,7 +165,7 @@
 
     def share(place):
         return copy(
-            FLOWS["share", place], img.at[img_rows(place, 0), :], img.at[img_rows(place, 1), :], other
+            "share", FLOWS["share", place], img.at[img_rows(place, 0), :], img.at[img_rows(place, 1), :], other
         )
 
     def go(kind, third, place):
@@ -177,9 +178,10 @@
 
     def come(third, place):
         for kind in ("img", "txt"):
-            gather(kind, third, place).wait_recv()
             if kind == "txt" and third == 0:
-                gather("ids", third, place).wait_recv()
+                both_here(FLOWS[kind, third, place])
+            else:
+                gather(kind, third, place).wait_recv()
             for later in onward(third, place):
                 go(kind, third, later)
 
@@ -280,7 +282,7 @@
 
     def give_back(place):
         return copy(
-            FLOWS["swap", 0] + place, dimg.at[img_rows(place, 1), :], swap.at[rows(place), :], other
+            "swap", FLOWS["swap", 0] + place, dimg.at[img_rows(place, 1), :], swap.at[rows(place), :], other
         )
 
     def slot(kind, third, place):
@@ -293,12 +295,14 @@
 
     def values(kind, third, place):
         s = slot(kind, third, place)
-        return copy(FLOWS[kind, third, place], sent.at[s], got.at[s], route(kind, third, place))
+        return copy(
+            "values", FLOWS[kind, third, place], sent.at[s], got.at[s], route(kind, third, place)
+        )
 
     def units(kind, third, place):
         s = slot(kind, third, place)
         return copy(
-            FLOWS[kind + "_s", third, place], sent_s.at[s], got_s.at[s], route(kind, third, place)
+            "units", FLOWS[kind, third, place], sent_s.at[s], got_s.at[s], route(kind, third, place)
         )
 
     def send(kind, third, place):
@@ -315,8 +319,7 @@
 
     def take(kind, third, place):
         s = slot(kind, third, place)
-        values(kind, third, place).wait_recv()
-        units(kind, third, place).wait_recv()
+        both_here(FLOWS[kind, third, place])
         unit = jnp.sum(jnp.where(eye, got_s[s, 0:1, :], 0.0), axis=1, keepdims=True)
         return got[s].astype(jnp.int32).astype(F32) * unit
 
@@ -340,7 +343,7 @@
         for stride in (1, 2, 3):
             launch(
                 lambda stride=stride: copy(
-                    FLOWS["loss", axis, stride], loss_tile.at[number], loss_got.at[number, here],
+                    "loss", FLOWS["loss", axis, stride], loss_tile.at[number], loss_got.at[number, here],
                     {axis: lax.rem(here + stride, 4)},
                 )
             )
@@ -349,7 +352,7 @@
         for stride in (1, 2, 3):
             source = lax.rem(here + 4 - stride, 4)
             copy(
-                FLOWS["loss", axis, stride], loss_tile.at[number], loss_got.at[number, source],
+                "loss", FLOWS["loss", axis, stride], loss_tile.at[number], loss_got.at[number, source],
                 {axis: lax.rem(here + stride, 4)},
             ).wait_recv()
         loss_tile[number + 1] = (loss_got[number, 0] + loss_got[number, 1]) + (
@@ -357,7 +360,7 @@
         )
 
     def loss_swap():
-        return copy(FLOWS["loss_core"], loss_tile.at[0], loss_got.at[0, 0], other)
+        return copy("loss_core", FLOWS["loss_core"], loss_tile.at[0], loss_got.at[0, 0], other)
 
     def two_back(place):
         pass_back(place)
@@ -429,20 +432,20 @@
 
     send_now("dtxt", 0b101)
     send_now("dtxt", 0b011)
-    loss_take("z", z, 1)
-    loss_send("x", x, 2)
     for third in THIRDS:
         for kind in ("dimg", "dtxt"):
             send(kind, third, firsts(third))
+    loss_take("z", z, 1)
+    loss_send("x", x, 2)
     for axis in range(3):
         merge(1 << axis)
         send_now("dimg", 1 << axis)
     merge(0)
-    loss_take("x", x, 2)
-    loss_send("y", y, 3)
     for third in THIRDS:
         for kind in ("dtxt", "dimg"):
             send(kind, third, 1 << ORDER[third][1])
+    loss_take("x", x, 2)
+    loss_send("y", y, 3)
     for third in THIRDS:
         for kind in ("dtxt", "dimg"):
             send(kind, third, 1 << ORDER[third][0])
@@ -459,8 +462,13 @@
         unit, recip = normalize(source[...])
         out[...] = project_back(unit, recip, grad)
 
-    for make in started:
-        make().wait_send()
+    sevens = pl.ds(0, 7 * ROWS)
+    for kind, every in (
+        ("img", txt.at[sevens, :]), ("txt", txt.at[sevens, :]), ("ids", ids.at[pl.ds(0, 7)]),
+        ("values", sent), ("units", sent_s), ("share", txt), ("swap", swap),
+        ("loss_core", loss_tile.at[0]), ("loss", sent_s.at[pl.ds(0, 9)]),
+    ):
+        copy(kind, 0, every, every, other).wait_send()
 
 
 def per_device(images, texts, lang_order, position, logit_scale, logit_bias):
@@ -498,8 +506,9 @@
             pltpu.VMEM((42, 8, rows), F32),
             pltpu.VMEM((5, 8, 128), F32),
             pltpu.VMEM((4, 4, 8, 128), F32),
+            pltpu.VMEM((200, 128), F32),
             pltpu.SemaphoreType.DMA((5,)),
-            pltpu.SemaphoreType.DMA((N_FLOW,)),
+            pltpu.SemaphoreType.DMA((len(SENT),)),
             pltpu.SemaphoreType.DMA((N_FLOW,)),
         ],
         compiler_params=pltpu.CompilerParams(

time: 76.1 us -> 74.8 us (0.983)
  Pallas kernels: 69.2 us -> 68 us
    pallas_call x1, Pallas kernels: 69.2 us -> 68 us  [per_device(): pl.pallas_call(kernel, out_shape=(jax.ShapeDtypeStruct((rows, width), F32...]
where the time goes in v8:
time: 74.8 us; the launch traced here: 74.5 us
  Pallas kernels  68 us (91%)
  between operations  3.67 us (5%)
  local copies, waits for them, and re-layouts  2.8 us (4%)
    pallas_call x1, Pallas kernels, per_device(): pl.pallas_call(kernel, out_shape=(jax.ShapeDtypeStruct((rows, width), F32...  68 us
    unnamed x4, local copies, waits for them, and re-layouts  2.8 us

profile of v8, /device:TPU:0, one launch (start us, length us, event | category | flops | bytes accessed | tf_op | source)
XLA Modules:
  0.0 74.5 jit_solution(4374329702532373019)
XLA Ops:
  1.9 68.0 %pair_grads.1 = (f32[128,1152]{1,0:T(8,128)}, f32[128,1152]{1,0:T(8,128)}, f32[1]{0:T(128)}) custom-call(bf16[128,1152]{1,0:T(8,128)(2,1)} %img_in.1, bf16[128,1152]{1,0:T(8,128)(2,1)} %txt_in.1, s32[1,128]{1,0:T(1,128)} %bitcast.1, f32[1]{0:T(128)S(6)} %copy.11.scale_ref, f32[1]{0:T(128)S(6)} %copy.12.bias_ref), custom_call_target="tpu_custom_call" | custom-call | tf_op jit(solution)/shard_map/pair_grads/pallas_call | solution.py:480
  69.9 0.0 copy-start
  69.9 2.0 %copy.13 = f32[128,1152]{1,0:T(8,128)} copy(f32[128,1152]{1,0:T(8,128)} %get-tuple-element.6) | data formatting | bytes 1179648
  71.9 0.0 copy-done
  71.9 0.8 %copy.14 = f32[128,1152]{1,0:T(8,128)} copy(f32[128,1152]{1,0:T(8,128)S(1)} %copy-done) | data formatting | bytes 1179648
Async XLA Ops:
  69.9 2.0 %copy-start = (f32[128,1152]{1,0:T(8,128)S(1)}, f32[128,1152]{1,0:T(8,128)}, u32[]{:S(2)}) copy-start(f32[128,1152]{1,0:T(8,128)} %get-tuple-element.7) | copy-start | bytes 1769476

commit v9 on v8

--- a/solution.py
+++ b/solution.py
@@ -79,7 +79,7 @@
     img_in, txt_in, ids_in, scale_ref, bias_ref,
     img_out, txt_out, loss_out,
     img_raw, txt_raw, ids_raw, scale_raw, bias_raw,
-    img, txt, ids, dimg, swap, dtxt, even, odd, sent, sent_s, got, got_s, loss_tile, loss_got,
+    img, txt, ids, dimg, swap, dtxt, even, odd, spare, sent, sent_s, got, got_s, loss_tile, loss_got,
     both, load_sem, send_sem, recv_sem,
 ):
     x, core = lax.axis_index("x"), lax.axis_index("core")
@@ -398,8 +398,6 @@
         5: all_here,
         10: far_back,
         11: lambda: two_back(5),
-        12: far_dimg,
-        13: partner_out,
     }
 
     def make(index, buffer):
@@ -419,15 +417,23 @@
                     pl.when(index == moment // 2)(event)
         return carry
 
-    lax.fori_loop(0, 7, step, 0)
-    make(jnp.int32(15), odd)
+    lax.fori_loop(0, 6, step, 0)
+    make(jnp.int32(13), odd)
+    use(jnp.int32(12), even)
+    far_dimg()
+    make(jnp.int32(14), even)
+    make(jnp.int32(15), spare)
     launch(loss_swap)
-    use(jnp.int32(14), even)
-    two_back(3)
+    use(jnp.int32(13), odd)
     loss_swap().wait_recv()
     loss_tile[1] = loss_tile[0] + loss_got[0, 0]
     loss_send("z", z, 1)
-    use(jnp.int32(15), odd)
+    partner_out()
+    use(jnp.int32(14), even)
+    two_back(3)
+    loss_take("z", z, 1)
+    loss_send("x", x, 2)
+    use(jnp.int32(15), spare)
     two_back(1)
 
     send_now("dtxt", 0b101)
@@ -435,17 +441,15 @@
     for third in THIRDS:
         for kind in ("dimg", "dtxt"):
             send(kind, third, firsts(third))
-    loss_take("z", z, 1)
-    loss_send("x", x, 2)
     for axis in range(3):
         merge(1 << axis)
         send_now("dimg", 1 << axis)
     merge(0)
+    loss_take("x", x, 2)
+    loss_send("y", y, 3)
     for third in THIRDS:
         for kind in ("dtxt", "dimg"):
             send(kind, third, 1 << ORDER[third][1])
-    loss_take("x", x, 2)
-    loss_send("y", y, 3)
     for third in THIRDS:
         for kind in ("dtxt", "dimg"):
             send(kind, third, 1 << ORDER[third][0])
@@ -500,6 +504,7 @@
             pltpu.VMEM((8 * rows, width), F32),
             pltpu.VMEM((4 * rows, 2 * rows), BF16),
             pltpu.VMEM((4 * rows, 2 * rows), BF16),
+            pltpu.VMEM((4 * rows, 2 * rows), BF16),
             pltpu.VMEM((42, rows, width // 3), jnp.int16),
             pltpu.VMEM((42, 8, rows), F32),
             pltpu.VMEM((42, rows, width // 3), jnp.int16),

time: 74.8 us -> 75 us (level)
  no operation moved by 1% of the time
where the time goes in v9:
time: 75 us; the launch traced here: 74.8 us
  Pallas kernels  68.4 us (91%)
  between operations  3.67 us (5%)
  local copies, waits for them, and re-layouts  2.8 us (4%)
    pallas_call x1, Pallas kernels, per_device(): pl.pallas_call(kernel, out_shape=(jax.ShapeDtypeStruct((rows, width), F32...  68.4 us
    unnamed x4, local copies, waits for them, and re-layouts  2.8 us

profile of v9, /device:TPU:0, one launch (start us, length us, event | category | flops | bytes accessed | tf_op | source)
XLA Modules:
  0.0 74.8 jit_solution(13342826050428624671)
XLA Ops:
  1.9 68.4 %pair_grads.1 = (f32[128,1152]{1,0:T(8,128)}, f32[128,1152]{1,0:T(8,128)}, f32[1]{0:T(128)}) custom-call(bf16[128,1152]{1,0:T(8,128)(2,1)} %img_in.1, bf16[128,1152]{1,0:T(8,128)(2,1)} %txt_in.1, s32[1,128]{1,0:T(1,128)} %bitcast.1, f32[1]{0:T(128)S(6)} %copy.11.scale_ref, f32[1]{0:T(128)S(6)} %copy.12.bias_ref), custom_call_target="tpu_custom_call" | custom-call | tf_op jit(solution)/shard_map/pair_grads/pallas_call | solution.py:484
  70.3 0.0 copy-start
  70.3 2.0 %copy.13 = f32[128,1152]{1,0:T(8,128)} copy(f32[128,1152]{1,0:T(8,128)} %get-tuple-element.6) | data formatting | bytes 1179648
  72.3 0.0 copy-done
  72.3 0.8 %copy.14 = f32[128,1152]{1,0:T(8,128)} copy(f32[128,1152]{1,0:T(8,128)S(1)} %copy-done) | data formatting | bytes 1179648
Async XLA Ops:
  70.3 2.0 %copy-start = (f32[128,1152]{1,0:T(8,128)S(1)}, f32[128,1152]{1,0:T(8,128)}, u32[]{:S(2)}) copy-start(f32[128,1152]{1,0:T(8,128)} %get-tuple-element.7) | copy-start | bytes 1769476

commit v10 on v8

--- a/solution.py
+++ b/solution.py
@@ -444,11 +444,11 @@
     for third in THIRDS:
         for kind in ("dtxt", "dimg"):
             send(kind, third, 1 << ORDER[third][1])
-    loss_take("x", x, 2)
-    loss_send("y", y, 3)
     for third in THIRDS:
         for kind in ("dtxt", "dimg"):
             send(kind, third, 1 << ORDER[third][0])
+    loss_take("x", x, 2)
+    loss_send("y", y, 3)
     for turn in (2, 1, 0):
         for third in THIRDS:
             for kind in ("dtxt", "dimg"):

time: 74.8 us -> 74.4 us (level)
  Pallas kernels: 68 us -> 66.9 us
    pallas_call x1, Pallas kernels: 68 us -> 66.9 us  [per_device(): pl.pallas_call(kernel, out_shape=(jax.ShapeDtypeStruct((rows, width), F32...]
where the time goes in v10:
time: 74.4 us; the launch traced here: 73.4 us
  Pallas kernels  66.9 us (90%)
  between operations  3.67 us (5%)
  local copies, waits for them, and re-layouts  2.8 us (4%)
    pallas_call x1, Pallas kernels, per_device(): pl.pallas_call(kernel, out_shape=(jax.ShapeDtypeStruct((rows, width), F32...  66.9 us
    unnamed x4, local copies, waits for them, and re-layouts  2.8 us

profile of v10, /device:TPU:0, one launch (start us, length us, event | category | flops | bytes accessed | tf_op | source)
XLA Modules:
  0.0 73.4 jit_solution(4152524314385880655)
XLA Ops:
  1.9 66.9 %pair_grads.1 = (f32[128,1152]{1,0:T(8,128)}, f32[128,1152]{1,0:T(8,128)}, f32[1]{0:T(128)}) custom-call(bf16[128,1152]{1,0:T(8,128)(2,1)} %img_in.1, bf16[128,1152]{1,0:T(8,128)(2,1)} %txt_in.1, s32[1,128]{1,0:T(1,128)} %bitcast.1, f32[1]{0:T(128)S(6)} %copy.11.scale_ref, f32[1]{0:T(128)S(6)} %copy.12.bias_ref), custom_call_target="tpu_custom_call" | custom-call | tf_op jit(solution)/shard_map/pair_grads/pallas_call | solution.py:480
  68.9 0.0 copy-start
  68.9 2.0 %copy.13 = f32[128,1152]{1,0:T(8,128)} copy(f32[128,1152]{1,0:T(8,128)} %get-tuple-element.6) | data formatting | bytes 1179648
  70.8 0.0 copy-done
  70.8 0.8 %copy.14 = f32[128,1152]{1,0:T(8,128)} copy(f32[128,1152]{1,0:T(8,128)S(1)} %copy-done) | data formatting | bytes 1179648
Async XLA Ops:
  68.9 2.0 %copy-start = (f32[128,1152]{1,0:T(8,128)S(1)}, f32[128,1152]{1,0:T(8,128)}, u32[]{:S(2)}) copy-start(f32[128,1152]{1,0:T(8,128)} %get-tuple-element.7) | copy-start | bytes 1769476

commit v11 on v10

--- a/solution.py
+++ b/solution.py
@@ -306,9 +306,10 @@
         )
 
     def send(kind, third, place):
-        for child in onward(third, place):
-            add(kind, third, child)
         ref = sum_ref(kind, third, place)
+        children = onward(third, place)
+        if children:
+            ref[...] += sum(take(kind, third, child) for child in children)
         s = slot(kind, third, place)
         top = jnp.maximum(jnp.max(jnp.abs(ref[...]), axis=1, keepdims=True), 1e-30)
         across_lanes = jnp.sum(jnp.where(eye, top * (1.0 / 32767.0), 0.0), axis=0, keepdims=True)
@@ -427,14 +428,15 @@
     loss_swap().wait_recv()
     loss_tile[1] = loss_tile[0] + loss_got[0, 0]
     loss_send("z", z, 1)
+    for third in THIRDS:
+        send("dimg", third, firsts(third))
     use(jnp.int32(15), odd)
     two_back(1)
 
     send_now("dtxt", 0b101)
     send_now("dtxt", 0b011)
     for third in THIRDS:
-        for kind in ("dimg", "dtxt"):
-            send(kind, third, firsts(third))
+        send("dtxt", third, firsts(third))
     loss_take("z", z, 1)
     loss_send("x", x, 2)
     for axis in range(3):

time: 74.4 us -> 75.1 us (level)
  no operation moved by 1% of the time
where the time goes in v11:
time: 75.1 us; the launch traced here: 74.1 us
  Pallas kernels  67.6 us (90%)
  between operations  3.67 us (5%)
  local copies, waits for them, and re-layouts  2.8 us (4%)
    pallas_call x1, Pallas kernels, per_device(): pl.pallas_call(kernel, out_shape=(jax.ShapeDtypeStruct((rows, width), F32...  67.6 us
    unnamed x4, local copies, waits for them, and re-layouts  2.8 us

profile of v11, /device:TPU:0, one launch (start us, length us, event | category | flops | bytes accessed | tf_op | source)
XLA Modules:
  0.0 74.1 jit_solution(1319994125058254295)
XLA Ops:
  1.9 67.6 %pair_grads.1 = (f32[128,1152]{1,0:T(8,128)}, f32[128,1152]{1,0:T(8,128)}, f32[1]{0:T(128)}) custom-call(bf16[128,1152]{1,0:T(8,128)(2,1)} %img_in.1, bf16[128,1152]{1,0:T(8,128)(2,1)} %txt_in.1, s32[1,128]{1,0:T(1,128)} %bitcast.1, f32[1]{0:T(128)S(6)} %copy.11.scale_ref, f32[1]{0:T(128)S(6)} %copy.12.bias_ref), custom_call_target="tpu_custom_call" | custom-call | tf_op jit(solution)/shard_map/pair_grads/pallas_call | solution.py:482
  69.5 0.0 copy-start
  69.6 2.0 %copy.13 = f32[128,1152]{1,0:T(8,128)} copy(f32[128,1152]{1,0:T(8,128)} %get-tuple-element.6) | data formatting | bytes 1179648
  71.5 0.0 copy-done
  71.5 0.8 %copy.14 = f32[128,1152]{1,0:T(8,128)} copy(f32[128,1152]{1,0:T(8,128)S(1)} %copy-done) | data formatting | bytes 1179648
Async XLA Ops:
  69.5 2.0 %copy-start = (f32[128,1152]{1,0:T(8,128)S(1)}, f32[128,1152]{1,0:T(8,128)}, u32[]{:S(2)}) copy-start(f32[128,1152]{1,0:T(8,128)} %get-tuple-element.7) | copy-start | bytes 1769476
